TPU v7x, 32 devices: a 4x2x2 block of a 4x4x8 slice. The times are simulated.
32 devices in a mesh: dp: 4 (over y, z), sp: 8 (over x, core).
Axes of the slice: x: 4, y: 2, z: 2, core: 2. Of those that a mesh axis runs over, the one named last changes fastest.
The devices are a block of a 4x4x8 slice.
Arguments:
- pair_rep: float32 [768, 192, 128], P(('dp', 'sp')), parts along dimension 0
- w_qkvg_s: bfloat16 [128, 512], replicated
- w_bias_s: bfloat16 [4, 128], replicated
- w_out_s: bfloat16 [128, 128], replicated
- w_qkvg_e: bfloat16 [128, 512], replicated
- w_bias_e: bfloat16 [4, 128], replicated
- w_out_e: bfloat16 [128, 128], replicated
- w_one: bfloat16 [128, 512], replicated
- w_two: bfloat16 [512, 128], replicated
Outputs:
- output: float32 [768, 192, 128], P(('dp', 'sp')), parts along dimension 0
There are 4 independent parts. A program takes and returns all parts, laid end to end along the dimension named above; an argument that names none is the same for every part.
All inputs are finite; a program needn't handle non-finite values.
Results may differ from a plain program's by a relative error of at most 0.0102889.
Values are sent between devices in bfloat16 or wider.
A program may use at most 768 MiB of HBM per device.

v0:
```python
import jax
import jax.numpy as jnp
from jax import lax
from jax.sharding import PartitionSpec as P

LN_EPS = 1e-5
SCORE_CAP = 2 ** 23


def layer_norm(values):
    vals_f = values.astype(jnp.float32)
    mean_c = jnp.mean(vals_f, axis=-1, keepdims=True)
    centered = vals_f - mean_c
    variance = jnp.mean(centered * centered, axis=-1, keepdims=True)
    return (centered * lax.rsqrt(variance + LN_EPS)).astype(jnp.bfloat16)


def project(normed, w_qkvg, num_heads):
    channels = w_qkvg.shape[0]
    projected = jnp.dot(normed, w_qkvg, preferred_element_type=jnp.float32)
    split_shape = normed.shape[:-1] + (num_heads, channels // num_heads)
    queries = projected[..., :channels].astype(jnp.bfloat16).reshape(split_shape)
    key_vecs = projected[..., channels:2 * channels].astype(jnp.bfloat16).reshape(split_shape)
    val_vecs = projected[..., 2 * channels:3 * channels].astype(jnp.bfloat16).reshape(split_shape)
    gate_vals = jax.nn.sigmoid(projected[..., 3 * channels:]).reshape(split_shape)
    return queries, key_vecs, val_vecs, gate_vals


def attend(queries, key_vecs, val_vecs, gate_vals, bias_full, w_out, score_form, mix_form):
    head_dim = queries.shape[-1]
    scores = jnp.einsum(score_form, queries, key_vecs, preferred_element_type=jnp.float32)
    scores = scores * head_dim ** -0.5 + bias_full.astype(jnp.float32)
    attn_prob = jax.nn.softmax(scores, axis=-1).astype(jnp.bfloat16)
    attn_out = jnp.einsum(mix_form, attn_prob, val_vecs, preferred_element_type=jnp.float32)
    gated_out = (attn_out * gate_vals).astype(jnp.bfloat16)
    merged = gated_out.reshape(gated_out.shape[:-2] + (w_out.shape[0],))
    return jnp.dot(merged, w_out, preferred_element_type=jnp.float32)


def transition(resid_in, w_one, w_two):
    hidden = jax.nn.relu(jnp.dot(layer_norm(resid_in), w_one, preferred_element_type=jnp.float32))
    return jnp.dot(hidden.astype(jnp.bfloat16), w_two, preferred_element_type=jnp.float32)


def block_size(total_len, per_item):
    return max(candidate for candidate in range(1, total_len + 1) if total_len % candidate == 0 and (candidate == 1 or candidate * per_item <= SCORE_CAP))


def solution(mesh):
    row_spec = P(('dp', 'sp'), None, None)

    def local_fn(pair_loc, w_qkvg_s, w_bias_s, w_out_s, w_qkvg_e, w_bias_e, w_out_e, w_one, w_two):
        num_rows, seq_len, channels = pair_loc.shape
        num_heads = w_bias_s.shape[0]
        blk_rows = block_size(num_rows, num_heads * seq_len * seq_len)
        normed = layer_norm(pair_loc)
        bias_loc = jnp.einsum('hc,jkc->hjk', w_bias_s, normed, preferred_element_type=jnp.float32).astype(jnp.bfloat16)
        bias_s = lax.all_gather(bias_loc, 'sp', axis=1, tiled=True)

        def start_block(block_idx):
            normed_blk = lax.dynamic_slice_in_dim(normed, block_idx * blk_rows, blk_rows, axis=0)
            queries, key_vecs, val_vecs, gate_vals = project(normed_blk, w_qkvg_s, num_heads)
            return attend(queries, key_vecs, val_vecs, gate_vals, bias_s, w_out_s, 'rjhd,rkhd->rhjk', 'rhjk,rkhd->rjhd')

        start_upd = lax.map(start_block, jnp.arange(num_rows // blk_rows))
        pair_one = pair_loc + start_upd.reshape(num_rows, seq_len, channels)
        col_major = lax.all_to_all(pair_one.astype(jnp.bfloat16), 'sp', 1, 0, tiled=True)
        normed_c = layer_norm(col_major)
        bias_loc_e = jnp.einsum('hc,kic->hik', w_bias_e, normed_c, preferred_element_type=jnp.float32).astype(jnp.bfloat16)
        bias_e = lax.all_gather(bias_loc_e, 'sp', axis=1, tiled=True)

        def end_block(block_idx):
            normed_blk = lax.dynamic_slice_in_dim(normed_c, block_idx * blk_rows, blk_rows, axis=1)
            pair_blk = lax.dynamic_slice_in_dim(col_major, block_idx * blk_rows, blk_rows, axis=1)
            queries, key_vecs, val_vecs, gate_vals = project(normed_blk, w_qkvg_e, num_heads)
            end_upd = attend(queries, key_vecs, val_vecs, gate_vals, bias_e, w_out_e, 'ijhd,kjhd->jhik', 'jhik,kjhd->ijhd')
            pair_two = pair_blk.astype(jnp.float32) + end_upd
            return (end_upd + transition(pair_two, w_one, w_two)).astype(jnp.bfloat16)

        delta_blocks = lax.map(end_block, jnp.arange(num_rows // blk_rows))
        delta_cols = jnp.moveaxis(delta_blocks, 0, 1).reshape(seq_len, num_rows, channels)
        delta_rows = lax.all_to_all(delta_cols, 'sp', 0, 1, tiled=True)
        return pair_one + delta_rows.astype(jnp.float32)

    return jax.shard_map(local_fn, mesh=mesh, in_specs=(row_spec, P(), P(), P(), P(), P(), P(), P(), P()), out_specs=row_spec, check_vma=False)
```

profile of v0, /device:TPU:81, one launch (start us, length us, event | category | flops | bytes accessed | tf_op | source)
XLA Modules:
  0.0 192.5 jit_solution(434759318078694117)
XLA Ops:
  0.0 0.0 copy-start
  0.0 0.0 copy-start.2
  0.0 0.0 copy-start.11
  0.0 2.7 %reduce_sum.76 = f32[24,192]{1,0:T(8,128)S(1)} reduce(f32[24,192,128]{2,1,0:T(8,128)} %param.9, f32[]{:T(128)} %constant.38.clone.1), dimensions={2}, to_apply=%region_0.0 | reduce | flops 585216 | bytes 2377732 | tf_op jit(solution)/shard_map/reduce_sum | solution.py:12
  2.7 0.0 copy-done.2
  2.7 1.7 multiply_reduce_fusion.1
  4.5 0.0 copy-done.11
  4.5 2.0 %fusion.33 = bf16[4,24,192]{2,0,1:T(4,128)(2,1)S(1)} fusion(f32[24,192,128]{2,1,0:T(8,128)S(1)} %copy-done.2, f32[24,192]{1,0:T(8,128)S(1)} %add_rsqrt_fusion.2, f32[24,192]{1,0:T(8,128)S(1)} %broadcast_multiply_fusion.2, bf16[4,128]{1,0:T(4,128)(2,1)S(1)} %copy-done.11), kind=kOutput, calls=%fused_computation.51 | convolution fusion | flops 6506496 | bytes 2434048 | tf_op jit(solution)/shard_map/hc,jkc->hjk/dot_general | solution.py:57
  6.5 15.0 %all_gather.6 = bf16[4,192,192]{2,0,1:T(4,128)(2,1)S(1)} all-gather(bf16[4,24,192]{2,0,1:T(4,128)(2,1)S(1)} %fusion.33), channel_id=1, replica_groups=mesh['dp'=4,'sp'=8] {'sp'}, dimensions={1}, use_global_device_ids=true | all-gather | bytes 331776 | tf_op jit(solution)/shard_map/all_gather | solution.py:58
  21.4 0.1 copy_convert_fusion.1
  21.5 1.2 copy.68
  22.7 0.0 copy-done
  22.7 4.7 %fusion.52 = (bf16[24,192,512]{2,1,0:T(8,128)(2,1)S(1)}, f32[24,192,512]{2,1,0:T(8,128)}) fusion(bf16[128,512]{1,0:T(8,128)(2,1)S(1)} %copy-done, f32[24,192,128]{2,1,0:T(8,128)S(1)} %copy-done.2, f32[24,192]{1,0:T(8,128)S(1)} %add_rsqrt_fusion.2, f32[24,192]{1,0:T(8,128)S(1)} %broadcast_multiply_fusion.2), kind=kOutput, calls=%fused_computation.77 | convolution fusion | flops 608108544 | bytes 16683008 | tf_op jit(solution)/shard_map/while/body/eval_jaxpr/dot_general | solution.py:20
  27.4 2.3 %fusion.51 = (bf16[24,192,128]{2,1,0:T(8,128)(2,1)}, bf16[24,192,128]{2,1,0:T(8,128)(2,1)}, bf16[24,192,128]{2,1,0:T(8,128)(2,1)}) fusion(bf16[24,192,512]{2,1,0:T(8,128)(2,1)S(1)} %get-tuple-element.47), kind=kLoop, calls=%fused_computation.76 | loop fusion | bytes 7077888 | tf_op jit(solution)/shard_map/while/body/eval_jaxpr/slice | solution.py:23
  29.7 2.5 %copy.66 = bf16[24,192,128]{1,2,0:T(8,128)(2,1)} copy(bf16[24,192,128]{2,1,0:T(8,128)(2,1)} %get-tuple-element.44) | data formatting | bytes 2359296 | tf_op jit(solution)/shard_map/while/body/eval_jaxpr/slice | solution.py:23
  32.2 2.5 %copy.65 = bf16[24,192,128]{1,2,0:T(8,128)(2,1)} copy(bf16[24,192,128]{2,1,0:T(8,128)(2,1)} %get-tuple-element.45) | data formatting | bytes 2359296 | tf_op jit(solution)/shard_map/while/body/eval_jaxpr/slice | solution.py:22
  34.8 2.6 %copy.64 = bf16[24,192,128]{1,2,0:T(8,128)(2,1)} copy(bf16[24,192,128]{2,1,0:T(8,128)(2,1)} %get-tuple-element.46) | data formatting | bytes 2359296 | tf_op jit(solution)/shard_map/while/body/eval_jaxpr/slice | solution.py:24
  37.3 3.7 %fusion.25 = f32[24,192,128]{2,1,0:T(8,128)} fusion(f32[24,192,512]{2,1,0:T(8,128)} %get-tuple-element.48), kind=kLoop, calls=%fused_computation.33 | loop fusion | flops 1769472 | bytes 4718592 | tf_op jit(solution)/shard_map/while/body/eval_jaxpr/div | solution.py:25
  41.0 3.5 %copy.70 = f32[24,192,128]{1,2,0:T(8,128)} copy(f32[24,192,128]{2,1,0:T(8,128)} %fusion.25) | data formatting | bytes 4718592 | tf_op jit(solution)/shard_map/while/body/eval_jaxpr/div | solution.py:25
  44.5 0.0 copy-done.6
  44.5 11.8 %fusion.53 = (f32[24,4,192]{2,1,0:T(4,128)S(1)}, f32[24,4,192,192]{2,3,1,0:T(8,128)}) fusion(bf16[24,192,4,32]{1,3,2,0:T(8,128)(2,1)} %bitcast.97, bf16[24,192,4,32]{1,3,2,0:T(8,128)(2,1)} %bitcast.95, f32[4,192,192]{1,2,0:T(8,128)S(1)} %copy-done.6), kind=kOutput, calls=%fused_computation.78 | convolution fusion | flops 240648384 | bytes 17178624 | tf_op jit(solution)/shard_map/while/body/eval_jaxpr/sub | solution.py:33
  56.4 0.0 copy-start.9
  56.4 9.6 %fusion.19 = bf16[24,192,4,32]{1,3,2,0:T(8,128)(2,1)S(1)} fusion(f32[24,192,4,32]{1,3,2,0:T(8,128)} %bitcast.92, bf16[24,192,4,32]{1,3,2,0:T(8,128)(2,1)} %bitcast.98, f32[24,4,192,192]{2,3,1,0:T(8,128)} %get-tuple-element.50, f32[24,4,192]{2,1,0:T(4,128)S(1)} %get-tuple-element.49), kind=kOutput, calls=%fused_computation.25 | convolution fusion | flops 234749952 | bytes 18948096 | tf_op jit(solution)/shard_map/while/body/eval_jaxpr/rhjk,rkhd->rjhd/dot_general | solution.py:34
  66.0 0.0 copy-done.9
  66.0 2.0 %fusion.54 = (bf16[24,192,128]{2,1,0:T(8,128)(2,1)S(1)}, f32[24,192,128]{2,1,0:T(8,128)}) fusion(f32[24,192,128]{2,1,0:T(8,128)S(1)} %copy-done.2, bf16[24,192,128]{1,2,0:T(8,128)(2,1)S(1)} %bitcast.94, bf16[128,128]{1,0:T(8,128)(2,1)S(1)} %copy-done.9), kind=kOutput, calls=%fused_computation.79 | convolution fusion | flops 152174592 | bytes 7110656 | tf_op jit(solution)/shard_map/while/body/eval_jaxpr/dot_general | solution.py:37
  68.0 0.8 copy.72
  68.8 20.3 %all_to_all.8 = bf16[24,192,128]{2,0,1:T(8,128)(2,1)S(1)} all-to-all(bf16[24,192,128]{2,0,1:T(8,128)(2,1)S(1)} %copy.72), channel_id=1, replica_groups=mesh['dp'=4,'sp'=8] {'sp'}, dimensions={1} | all-to-all | bytes 2359296 | tf_op jit(solution)/shard_map/all_to_all | solution.py:67
  89.0 0.2 convert.20
  89.2 0.2 copy.73
  89.4 0.0 copy-start.14
  89.4 0.7 bitcast_reduce_fusion
  90.1 1.4 fusion.27
  91.6 0.0 copy-done.14
  91.6 2.9 %fusion.32 = bf16[4,24,192]{1,0,2:T(4,128)(2,1)S(1)} fusion(f32[192,24,128]{2,1,0:T(8,128)S(1)} %bitcast.86, f32[192,24]{1,0:T(8,128)S(1)} %bitcast.104, f32[192,24]{1,0:T(8,128)S(1)} %bitcast.102, bf16[4,128]{1,0:T(4,128)(2,1)S(1)} %copy-done.14), kind=kOutput, calls=%fused_computation.49 | convolution fusion | flops 6506496 | bytes 2434048 | tf_op jit(solution)/shard_map/hc,kic->hik/dot_general | solution.py:69
  94.4 0.2 copy.77
  94.6 13.8 %all_gather.7 = bf16[4,192,192]{2,0,1:T(4,128)(2,1)S(1)} all-gather(bf16[4,24,192]{2,0,1:T(4,128)(2,1)S(1)} %copy.77), channel_id=1, replica_groups=mesh['dp'=4,'sp'=8] {'sp'}, dimensions={1}, use_global_device_ids=true | all-gather | bytes 331776 | tf_op jit(solution)/shard_map/all_gather | solution.py:70
  108.4 0.1 copy_convert_fusion
  108.5 1.2 copy.79
  109.7 0.0 copy-done.8
  109.7 4.7 %fusion.55 = (bf16[192,24,512]{2,1,0:T(8,128)(2,1)S(1)}, f32[192,24,512]{2,1,0:T(8,128)}) fusion(bf16[128,512]{1,0:T(8,128)(2,1)S(1)} %copy-done.8, f32[192,24,128]{2,1,0:T(8,128)S(1)} %bitcast.87, f32[192,24]{1,0:T(8,128)S(1)} %bitcast.105, f32[192,24]{1,0:T(8,128)S(1)} %bitcast.103), kind=kOutput, calls=%fused_computation.80 | convolution fusion | flops 608108544 | bytes 16683008 | tf_op jit(solution)/shard_map/while/body/eval_jaxpr/dot_general | solution.py:20
  114.4 2.0 %fusion.50 = (bf16[192,24,128]{2,1,0:T(8,128)(2,1)}, bf16[192,24,128]{2,1,0:T(8,128)(2,1)}, bf16[192,24,128]{2,1,0:T(8,128)(2,1)}) fusion(bf16[192,24,512]{2,1,0:T(8,128)(2,1)S(1)} %get-tuple-element.64), kind=kLoop, calls=%fused_computation.75 | loop fusion | bytes 7077888 | tf_op jit(solution)/shard_map/while/body/eval_jaxpr/slice | solution.py:23
  116.4 2.9 %copy.76 = bf16[192,24,128]{0,2,1:T(8,128)(2,1)} copy(bf16[192,24,128]{2,1,0:T(8,128)(2,1)} %get-tuple-element.32) | data formatting | bytes 2359296 | tf_op jit(solution)/shard_map/while/body/eval_jaxpr/slice | solution.py:23
  119.3 2.8 %copy.75 = bf16[192,24,128]{0,2,1:T(8,128)(2,1)} copy(bf16[192,24,128]{2,1,0:T(8,128)(2,1)} %get-tuple-element.42) | data formatting | bytes 2359296 | tf_op jit(solution)/shard_map/while/body/eval_jaxpr/slice | solution.py:22
  122.2 2.9 %copy.74 = bf16[192,24,128]{0,2,1:T(8,128)(2,1)} copy(bf16[192,24,128]{2,1,0:T(8,128)(2,1)} %get-tuple-element.43) | data formatting | bytes 2359296 | tf_op jit(solution)/shard_map/while/body/eval_jaxpr/slice | solution.py:24
  125.1 3.7 %fusion.22 = f32[192,24,128]{2,1,0:T(8,128)} fusion(f32[192,24,512]{2,1,0:T(8,128)} %get-tuple-element.65), kind=kLoop, calls=%fused_computation.29 | loop fusion | flops 1769472 | bytes 4718592 | tf_op jit(solution)/shard_map/while/body/eval_jaxpr/div | solution.py:25
  128.7 3.7 %copy.81 = f32[192,24,128]{0,2,1:T(8,128)} copy(f32[192,24,128]{2,1,0:T(8,128)} %fusion.22) | data formatting | bytes 4718592 | tf_op jit(solution)/shard_map/while/body/eval_jaxpr/div | solution.py:25
  132.4 0.0 copy-done.7
  132.4 11.8 %fusion.56 = (f32[24,4,192]{2,1,0:T(4,128)S(1)}, f32[24,4,192,192]{2,3,1,0:T(8,128)}) fusion(bf16[192,24,4,32]{0,3,2,1:T(8,128)(2,1)} %bitcast.99, bf16[192,24,4,32]{0,3,2,1:T(8,128)(2,1)} %bitcast.96, f32[4,192,192]{1,2,0:T(8,128)S(1)} %copy-done.7), kind=kOutput, calls=%fused_computation.81 | convolution fusion | flops 240648384 | bytes 17178624 | tf_op jit(solution)/shard_map/while/body/eval_jaxpr/sub | solution.py:33
  144.2 10.8 %fusion.18 = bf16[192,24,4,32]{0,3,2,1:T(8,128)(2,1)} fusion(f32[192,24,4,32]{0,3,2,1:T(8,128)} %bitcast.93, bf16[192,24,4,32]{0,3,2,1:T(8,128)(2,1)} %bitcast.100, f32[24,4,192,192]{2,3,1,0:T(8,128)} %get-tuple-element.67, f32[24,4,192]{2,1,0:T(4,128)S(1)} %get-tuple-element.66), kind=kOutput, calls=%fused_computation.23 | convolution fusion | flops 234749952 | bytes 18948096 | tf_op jit(solution)/shard_map/while/body/eval_jaxpr/jhik,kjhd->ijhd/dot_general | solution.py:34
  155.0 2.6 %copy.82 = bf16[192,24,128]{2,1,0:T(8,128)(2,1)} copy(bf16[192,24,128]{0,2,1:T(8,128)(2,1)} %bitcast.101) | data formatting | bytes 2359296 | tf_op jit(solution)/shard_map/while/body/eval_jaxpr/reshape | solution.py:36
  157.7 0.0 copy-done.10
  157.7 3.4 %fusion.49 = (f32[192,24]{1,0:T(8,128)S(1)}, f32[192,24,128]{2,1,0:T(8,128)S(1)}, f32[192,24,128]{2,1,0:T(8,128)}) fusion(f32[192,24,128]{2,1,0:T(8,128)S(1)} %bitcast.88, bf16[192,24,128]{2,1,0:T(8,128)(2,1)} %copy.82, bf16[128,128]{1,0:T(8,128)(2,1)S(1)} %copy-done.10), kind=kOutput, calls=%fused_computation.74 | convolution fusion | flops 152169984 | bytes 8308736 | tf_op jit(solution)/shard_map/while/body/eval_jaxpr/dot_general | solution.py:37
  161.1 1.4 copy-done.4
  162.5 1.4 multiply_reduce_fusion
  164.0 0.0 copy-done.5
  164.0 0.0 copy-done.12
  164.0 0.0 copy-done.13
  164.0 5.2 %add_convert_fusion = bf16[192,24,128]{2,1,0:T(8,128)(2,1)} fusion(f32[192,24,128]{2,1,0:T(8,128)S(1)} %copy-done.5, f32[192,24,128]{2,1,0:T(8,128)} %copy-done.4, f32[192,24]{1,0:T(8,128)S(1)} %add_rsqrt_fusion, f32[192,24]{1,0:T(8,128)S(1)} %broadcast_multiply_fusion, bf16[512,128]{1,0:T(8,128)(2,1)S(1)} %copy-done.12, bf16[128,512]{1,0:T(8,128)(2,1)S(1)} %copy-done.13), kind=kOutput, calls=%fused_computation.39 | convolution fusion | flops 1215627264 | bytes 6197248 | tf_op jit(solution)/shard_map/while/body/eval_jaxpr/dot_general | solution.py:42
  169.2 20.0 %all_to_all.9 = bf16[192,24,128]{2,1,0:T(8,128)(2,1)S(1)} all-to-all(bf16[192,24,128]{2,1,0:T(8,128)(2,1)} %add_convert_fusion), channel_id=1, replica_groups=mesh['dp'=4,'sp'=8] {'sp'}, dimensions={0} | all-to-all | bytes 2359296 | tf_op jit(solution)/shard_map/all_to_all | solution.py:82
  189.1 0.3 copy.83
  189.4 0.0 copy-start.1
  189.4 1.4 copy-done.3
  190.8 1.7 bitcast_add_fusion
  192.5 0.0 copy-done.1
  (15 shorter events, 0.1 us)
Async XLA Ops:
  0.0 22.7 %copy-start = (bf16[128,512]{1,0:T(8,128)(2,1)S(1)}, bf16[128,512]{1,0:T(8,128)(2,1)}, u32[]{:S(2)}) copy-start(bf16[128,512]{1,0:T(8,128)(2,1)} %param.10) | copy-start | bytes 393220
  0.0 2.7 %copy-start.2 = (f32[24,192,128]{2,1,0:T(8,128)S(1)}, f32[24,192,128]{2,1,0:T(8,128)}, u32[]{:S(2)}) copy-start(f32[24,192,128]{2,1,0:T(8,128)} %param.9) | copy-start | bytes 7077892
  0.0 4.5 %copy-start.11 = (bf16[4,128]{1,0:T(4,128)(2,1)S(1)}, bf16[4,128]{1,0:T(4,128)(2,1)}, u32[]{:S(2)}) copy-start(bf16[4,128]{1,0:T(4,128)(2,1)} %param.11) | copy-start | bytes 3076
  41.0 3.5 %copy-start.6 = (f32[4,192,192]{1,2,0:T(8,128)S(1)}, f32[4,192,192]{1,2,0:T(8,128)}, u32[]{:S(2)}) copy-start(f32[4,192,192]{1,2,0:T(8,128)} %copy.68) | copy-start | bytes 1769476
  56.4 9.6 %copy-start.9 = (bf16[128,128]{1,0:T(8,128)(2,1)S(1)}, bf16[128,128]{1,0:T(8,128)(2,1)}, u32[]{:S(2)}) copy-start(bf16[128,128]{1,0:T(8,128)(2,1)} %param.12) | copy-start | bytes 98308
  89.4 2.2 %copy-start.14 = (bf16[4,128]{1,0:T(4,128)(2,1)S(1)}, bf16[4,128]{1,0:T(4,128)(2,1)}, u32[]{:S(2)}) copy-start(bf16[4,128]{1,0:T(4,128)(2,1)} %param.14) | copy-start | bytes 3076
  94.4 15.3 %copy-start.8 = (bf16[128,512]{1,0:T(8,128)(2,1)S(1)}, bf16[128,512]{1,0:T(8,128)(2,1)}, u32[]{:S(2)}) copy-start(bf16[128,512]{1,0:T(8,128)(2,1)} %param.13) | copy-start | bytes 393220
  128.7 3.7 %copy-start.7 = (f32[4,192,192]{1,2,0:T(8,128)S(1)}, f32[4,192,192]{1,2,0:T(8,128)}, u32[]{:S(2)}) copy-start(f32[4,192,192]{1,2,0:T(8,128)} %copy.79) | copy-start | bytes 1769476
  155.0 2.6 %copy-start.10 = (bf16[128,128]{1,0:T(8,128)(2,1)S(1)}, bf16[128,128]{1,0:T(8,128)(2,1)}, u32[]{:S(2)}) copy-start(bf16[128,128]{1,0:T(8,128)(2,1)} %param.15) | copy-start | bytes 98308
  161.1 1.4 copy-start.4
  161.1 2.9 %copy-start.5 = (f32[192,24,128]{2,1,0:T(8,128)S(1)}, f32[192,24,128]{2,1,0:T(8,128)}, u32[]{:S(2)}) copy-start(f32[192,24,128]{2,1,0:T(8,128)} %get-tuple-element.68) | copy-start | bytes 7077892
  161.1 2.9 %copy-start.12 = (bf16[512,128]{1,0:T(8,128)(2,1)S(1)}, bf16[512,128]{1,0:T(8,128)(2,1)}, u32[]{:S(2)}) copy-start(bf16[512,128]{1,0:T(8,128)(2,1)} %param.17) | copy-start | bytes 393220
  161.1 2.9 %copy-start.13 = (bf16[128,512]{1,0:T(8,128)(2,1)S(1)}, bf16[128,512]{1,0:T(8,128)(2,1)}, u32[]{:S(2)}) copy-start(bf16[128,512]{1,0:T(8,128)(2,1)} %param.16) | copy-start | bytes 393220
  189.1 1.7 copy-start.3
  189.4 3.1 %copy-start.1 = (bf16[128,512]{1,0:T(8,128)(2,1)S(1)}, bf16[128,512]{1,0:T(8,128)(2,1)}, u32[]{:S(2)}) copy-start(bf16[128,512]{1,0:T(8,128)(2,1)} %param.10) | copy-start | bytes 393220
where the time goes:
time: 193 us; the launch traced here: 192 us
  matrix products  69 us (36%)
  blocking collectives  69 us (36%)
  local copies, waits for them, and re-layouts  36.9 us (19%)
  other arithmetic  17.3 us (9%)
    sub x2, matrix products, attend(): attn_prob = jax.nn.softmax(scores, axis=-1).astype(jnp.bfloat16)  23.7 us
    dot_general x2, matrix products, attend(): jnp.einsum(mix_form, attn_prob, val_vecs, preferred_element_type=jnp.floa...  20.4 us
    all_to_all x1, blocking collectives, local_fn(): lax.all_to_all(pair_one.astype(jnp.bfloat16), 'sp', 1, 0, tiled=True)  20.3 us
    all_to_all x1, blocking collectives, local_fn(): delta_rows = lax.all_to_all(delta_cols, 'sp', 0, 1, tiled=True)  20 us
    all_gather x1, blocking collectives, local_fn(): bias_s = lax.all_gather(bias_loc, 'sp', axis=1, tiled=True)  15 us
    all_gather x1, blocking collectives, local_fn(): bias_e = lax.all_gather(bias_loc_e, 'sp', axis=1, tiled=True)  13.8 us
    slice x4, local copies, waits for them, and re-layouts, project(): projected[..., channels:2 * channels].astype(jnp.bfloat16)  9.71 us
    dot_general x2, matrix products, project(): projected = jnp.dot(normed, w_qkvg, preferred_element_type=jnp.float32)  9.44 us

commit v1 on v0

v1 whole, which is shorter than its diff:
```python
import functools

import jax
import jax.numpy as jnp
from jax import lax
from jax.experimental import pallas as pl
from jax.experimental.pallas import tpu as pltpu
from jax.sharding import PartitionSpec as P

LN_EPS = 1e-5
LANES = 128
F32, BF16 = jnp.float32, jnp.bfloat16


def layer_norm(vals):
    mean = jnp.mean(vals, axis=-1, keepdims=True)
    centered = vals - mean
    var = jnp.mean(centered * centered, axis=-1, keepdims=True)
    return (centered * lax.rsqrt(var + LN_EPS)).astype(BF16)


def mm(lhs, rhs, contract=((1,), (0,))):
    return lax.dot_general(lhs, rhs, (contract, ((), ())), preferred_element_type=F32)


def loop(count, body, unroll=1):
    def step(idx, carry):
        for sub in range(unroll):
            body(idx * unroll + sub)
        return carry

    lax.fori_loop(0, count // unroll, step, 0)


def kernel(cfg, z_ref, wqs_ref, wbs_ref, wos_ref, wqe_ref, wbe_ref, woe_ref, w1_ref, w2_ref, out_ref,
           z1, flat, norm, w_t, w_b, qmask, v_t, gate_t, keys, bias_rows, bias_out, bias_in, bias_t,
           h_out, h_in, d_out, d_in, out_sem, bias_sem, h_sem, d_sem):
    group, rows, seq, chan, heads, axis = cfg
    dim = chan // heads
    me = lax.axis_index(axis)
    tail = seq - LANES
    sub = rows // 8
    scale = dim ** -0.5

    barrier = pltpu.get_barrier_semaphore()
    for off in range(1, group):
        pl.semaphore_signal(barrier, inc=1, device_id={axis: lax.rem(me + off, group)}, device_id_type=pl.DeviceIdType.MESH)

    lane = lax.broadcasted_iota(jnp.int32, (1, LANES), 1)
    low = lane < tail

    def doubled(rows_in):
        return jnp.concatenate([rows_in, rows_in[LANES:seq]], axis=0)

    def peers(start):
        for off in range(1, group):
            start(lax.rem(me + off, group))

    def remote(src, dst, recv, dst_dev):
        return pltpu.make_async_remote_copy(src_ref=src, dst_ref=dst, send_sem=out_sem, recv_sem=recv,
                                            device_id={axis: dst_dev}, device_id_type=pl.DeviceIdType.MESH)

    def wait_recv(ref, sem):
        part = ref.at[pl.ds(0, group - 1)]
        pltpu.make_async_remote_copy(src_ref=part, dst_ref=part, send_sem=out_sem, recv_sem=sem,
                                     device_id={axis: me}, device_id_type=pl.DeviceIdType.MESH).wait_recv()

    def wait_send(ref):
        part = ref.at[pl.ds(0, group - 1)]
        pltpu.make_async_remote_copy(src_ref=part, dst_ref=part, send_sem=out_sem, recv_sem=out_sem,
                                     device_id={axis: me}, device_id_type=pl.DeviceIdType.MESH).wait_send()

    def load_weights(wq_ref, wb_ref):
        for dst, src in ((0, 0), (1, 2), (2, 3)):
            w_t[pl.ds(dst * chan, chan), :] = wq_ref[:, pl.ds(src * chan, chan)].T
        w_b[...] = jnp.zeros(w_b.shape, w_b.dtype)
        w_b[pl.ds(0, heads), :] = wb_ref[...].astype(F32)

    def norm_and_bias(read, phase, first_send):
        wb = w_b[...].astype(BF16)

        def row(r):
            u = layer_norm(read(r))
            norm[r] = u
            b = mm(wb, doubled(u), ((1,), (1,)))
            for pair in range(heads // 2):
                b0, b1 = b[2 * pair:2 * pair + 1], b[2 * pair + 1:2 * pair + 2]
                bias_rows[pair, 0, pl.ds(r, 1), :] = b0[:, :LANES]
                bias_rows[pair, 1, pl.ds(r, 1), :] = b1[:, :LANES]
                bias_rows[pair, 2, pl.ds(r, 1), :] = jnp.where(low, b0[:, LANES:], b1[:, LANES:])

        loop(rows, row, 4)
        rounded = bias_rows[...].astype(BF16).reshape(bias_out.shape[1:])
        bias_out[phase] = rounded
        bias_in[phase, me] = rounded
        first_send()
        peers(lambda d: remote(bias_out.at[phase], bias_in.at[phase, me], bias_sem.at[phase], d).start())

    def project(wq_ref):
        def row(r):
            u = norm[r]
            keys[r] = mm(u, wq_ref[:, pl.ds(chan, chan)]).astype(BF16)
            proj = mm(w_t[...], doubled(u), ((1,), (1,)))
            q, v, gl = proj[:chan], proj[chan:2 * chan], proj[2 * chan:]
            qmask[r, :, pl.ds(0, LANES)] = q[:, :LANES].astype(BF16)
            for h in range(heads):
                part = q[h * dim:(h + 1) * dim, LANES:]
                keep = low if h % 2 == 0 else jnp.logical_not(low)
                qmask[r, pl.ds(h * dim, dim), pl.ds(LANES, LANES)] = jnp.where(keep, part, 0.0).astype(BF16)
            v_t[r] = v[:, :seq].astype(BF16)
            gate_t[r] = jax.nn.sigmoid(gl)

        loop(rows, row, 2)

    def spread_bias(phase):
        wait_recv(bias_in.at[phase], bias_sem.at[phase])
        for pair in range(heads // 2):
            t0, t1, t2 = [doubled(bias_in[phase, :, pair, t].astype(F32).reshape(group * rows, LANES)).T for t in range(3)]
            even = jnp.concatenate([t0, t2[:tail]], axis=0)
            odd = jnp.concatenate([t1, t2[tail:]], axis=0)
            bias_t[pair, :, pl.ds(0, LANES)] = even[:, :LANES]
            bias_t[pair, :, pl.ds(LANES, LANES)] = odd[:, :LANES]
            bias_t[2, :, pl.ds(pair * LANES, LANES)] = jnp.where(low, even[:, LANES:], odd[:, LANES:])

    def attention(r, wo):
        key, qm, vt, gate = keys[r], qmask[r], v_t[r], gate_t[r]
        zero = jnp.zeros((dim, LANES), BF16)
        zero2 = jnp.zeros((2 * dim, LANES), BF16)
        zero4 = jnp.zeros((2 * dim, 2 * LANES), BF16)

        def pair_rhs(pair):
            a = qm[2 * pair * dim:(2 * pair + 1) * dim, :LANES]
            b = qm[(2 * pair + 1) * dim:(2 * pair + 2) * dim, :LANES]
            return jnp.concatenate([jnp.concatenate([a, zero], axis=1), jnp.concatenate([zero, b], axis=1)], axis=0)

        rhs = [jnp.concatenate([pair_rhs(0), zero4], axis=0), jnp.concatenate([zero4, pair_rhs(1)], axis=0),
               jnp.concatenate([jnp.concatenate([qm[:2 * dim, LANES:], zero2], axis=1),
                                jnp.concatenate([zero2, qm[2 * dim:, LANES:]], axis=1)], axis=0)]
        values = [vt[:2 * dim], vt[2 * dim:], vt]
        mixed = []
        for t in range(3):
            s = mm(key, rhs[t]) * scale + bias_t[t]
            e = jnp.exp(s - jnp.max(s, axis=0, keepdims=True))
            total = jnp.sum(e, axis=0, keepdims=True)
            mixed.append(mm(values[t], e.astype(BF16)) * (1.0 / total))
        main = jnp.concatenate([mixed[0][:dim, :LANES], mixed[0][dim:, LANES:], mixed[1][:dim, :LANES], mixed[1][dim:, LANES:]], axis=0)
        rest = []
        for h in range(heads):
            part = mixed[2][h * dim:(h + 1) * dim, (h // 2) * LANES:(h // 2 + 1) * LANES] * gate[h * dim:(h + 1) * dim, LANES:]
            rest.append(jnp.where(low if h % 2 == 0 else jnp.logical_not(low), part, 0.0))
        main = (main * gate[:, :LANES]).astype(BF16)
        rest = jnp.concatenate(rest, axis=0).astype(BF16)
        upd = mm(jnp.concatenate([main.T, rest.T], axis=0), wo)
        return jnp.concatenate([upd[:LANES], upd[LANES:LANES + tail] + upd[LANES + tail:]], axis=0)

    def send_row(r, src, dst, sem):
        mine = pl.ds(me * sub, sub)
        dst[me, r] = src[r, mine]
        peers(lambda d: remote(src.at[r, pl.ds(d * sub, sub)], dst.at[me, r], sem, d).start())

    def unpack(src):
        def part(d):
            flat[pl.ds(d * rows * rows, rows * rows), :] = src[d].astype(F32).reshape(rows * rows, chan)

        loop(group, part)

    load_weights(wqs_ref, wbs_ref)
    norm_and_bias(lambda r: z_ref[r], 0, lambda: pl.semaphore_wait(barrier, group - 1))
    project(wqs_ref)
    spread_bias(0)

    def start_row(r):
        new = z_ref[r] + attention(r, wos_ref[...])
        z1[r] = new
        h_out[r] = new.astype(BF16).reshape(seq // 8, 8, chan)
        send_row(r, h_out, h_in, h_sem)

    loop(rows, start_row, 2)

    load_weights(wqe_ref, wbe_ref)
    wait_recv(h_in, h_sem)
    unpack(h_in)
    column = lambda c: flat[pl.ds(c, seq, stride=rows), :]
    norm_and_bias(column, 1, lambda: None)
    project(wqe_ref)
    spread_bias(1)

    def end_row(c):
        upd = attention(c, woe_ref[...])
        hidden = jnp.maximum(mm(layer_norm(column(c) + upd), w1_ref[...]), 0.0).astype(BF16)
        delta = upd + mm(hidden, w2_ref[...])
        d_out[c] = delta.astype(BF16).reshape(seq // 8, 8, chan)
        send_row(c, d_out, d_in, d_sem)

    loop(rows, end_row, 2)
    wait_recv(d_in, d_sem)
    unpack(d_in)

    def final(r):
        out_ref[r] = z1[r] + flat[pl.ds(r, seq, stride=rows), :]

    loop(rows, final, 2)
    for phase in range(2):
        for _ in range(group - 1):
            remote(bias_out.at[phase], bias_in.at[phase, me], bias_sem.at[phase], me).wait_send()
    wait_send(h_in)
    wait_send(d_in)


def solution(mesh):
    axis = 'sp'
    group = mesh.shape[axis]
    row_spec = P(('dp', 'sp'), None, None)

    def local_fn(pair_loc, w_qkvg_s, w_bias_s, w_out_s, w_qkvg_e, w_bias_e, w_out_e, w_one, w_two):
        rows, seq, chan = pair_loc.shape
        heads = w_bias_s.shape[0]
        sub = rows // 8
        packed = 2 * LANES
        vmem = pl.BlockSpec(memory_space=pltpu.VMEM)
        scratch = [
            pltpu.VMEM((rows, seq, chan), F32),
            pltpu.VMEM((rows * seq, chan), F32),
            pltpu.VMEM((rows, seq, chan), BF16),
            pltpu.VMEM((3 * chan, chan), BF16),
            pltpu.VMEM((16, chan), F32),
            pltpu.VMEM((rows, chan, packed), BF16),
            pltpu.VMEM((rows, chan, seq), BF16),
            pltpu.VMEM((rows, chan, packed), F32),
            pltpu.VMEM((rows, seq, chan), BF16),
            pltpu.VMEM((heads // 2, 3, rows, LANES), F32),
            pltpu.VMEM((2, heads // 2, 3, sub, 8, LANES), BF16),
            pltpu.VMEM((2, group, heads // 2, 3, sub, 8, LANES), BF16),
            pltpu.VMEM((3, seq, packed), F32),
            pltpu.VMEM((rows, seq // 8, 8, chan), BF16),
            pltpu.VMEM((group, rows, sub, 8, chan), BF16),
            pltpu.VMEM((rows, seq // 8, 8, chan), BF16),
            pltpu.VMEM((group, rows, sub, 8, chan), BF16),
            pltpu.SemaphoreType.DMA,
            pltpu.SemaphoreType.DMA((2,)),
            pltpu.SemaphoreType.DMA,
            pltpu.SemaphoreType.DMA,
        ]
        return pl.pallas_call(
            functools.partial(kernel, (group, rows, seq, chan, heads, axis)),
            out_shape=jax.ShapeDtypeStruct(pair_loc.shape, F32),
            in_specs=[vmem] * 9,
            out_specs=vmem,
            scratch_shapes=scratch,
            compiler_params=pltpu.CompilerParams(collective_id=0, has_side_effects=True, vmem_limit_bytes=60 * 2 ** 20),
        )(pair_loc, w_qkvg_s, w_bias_s, w_out_s, w_qkvg_e, w_bias_e, w_out_e, w_one, w_two)

    return jax.shard_map(local_fn, mesh=mesh, in_specs=(row_spec, P(), P(), P(), P(), P(), P(), P(), P()), out_specs=row_spec, check_vma=False)
```

time: 193 us -> 97.5 us (0.51)
  Pallas kernels: 0 us -> 94 us
  matrix products: 69 us -> 0 us
  blocking collectives: 69 us -> 0 us
  local copies, waits for them, and re-layouts: 36.9 us -> 3.3 us
  other arithmetic: 17.3 us -> 0 us
    pallas_call x0 -> x1, Pallas kernels: none -> 94 us  [local_fn(): pl.pallas_call(functools.partial(kernel, (group, rows, seq, chan, heads,...]
    dot_general x9 -> x0, matrix products: 45.3 us -> none  [the longest x2 20.4 us: attend(): jnp.einsum(mix_form, attn_prob, val_vecs, preferred_element_type=jnp.floa...]
    all_to_all x2 -> x0, blocking collectives: 40.2 us -> none  [the longest x1 20.3 us: local_fn(): lax.all_to_all(pair_one.astype(jnp.bfloat16), 'sp', 1, 0, tiled=True)]
    all_gather x2 -> x0, blocking collectives: 28.8 us -> none  [the longest x1 15 us: local_fn(): bias_s = lax.all_gather(bias_loc, 'sp', axis=1, tiled=True)]
    sub x2 -> x0, matrix products: 23.7 us -> none  [attend(): attn_prob = jax.nn.softmax(scores, axis=-1).astype(jnp.bfloat16)]
    slice x8 -> x0, local copies, waits for them, and re-layouts: 20.5 us -> none  [the longest x4 9.71 us: project(): projected[..., channels:2 * channels].astype(jnp.bfloat16)]
    reduce_sum x5 -> x0, other arithmetic: 7.96 us -> none  [the longest x3 4.58 us: layer_norm(): variance = jnp.mean(centered * centered, axis=-1, keepdims=True)]
    div x5 -> x0, other arithmetic: 7.39 us -> none  [the longest x2 7.37 us: project(): jax.nn.sigmoid(projected[..., 3 * channels:]).reshape(split_shape)]
where the time goes in v1:
time: 97.5 us; the launch traced here: 97.3 us
  Pallas kernels  94 us (96%)
  local copies, waits for them, and re-layouts  3.3 us (3%)
    pallas_call x1, Pallas kernels, local_fn(): pl.pallas_call(functools.partial(kernel, (group, rows, seq, chan, heads,...  94 us
    unnamed x1, local copies, waits for them, and re-layouts  3.3 us

profile of v1, /device:TPU:81, one launch (start us, length us, event | category | flops | bytes accessed | tf_op | source)
XLA Modules:
  0.0 97.3 jit_solution(9739974144111640209)
XLA Ops:
  0.0 94.0 %shard_map.91 = f32[24,192,128]{2,1,0:T(8,128)} custom-call(f32[24,192,128]{2,1,0:T(8,128)} %z_ref.1, bf16[128,512]{1,0:T(8,128)(2,1)} %wqs_ref.1, bf16[4,128]{1,0:T(4,128)(2,1)} %wbs_ref.1, bf16[128,128]{1,0:T(8,128)(2,1)} %wos_ref.1, bf16[128,512]{1,0:T(8,128)(2,1)} %wqe_ref.1, bf16[4,128]{1,0:T(4,128)(2,1)} %wbe_ref.1, bf16[128,128]{1,0:T(8,128)(2,1)} %woe_ref.1, ...), custom_call_target="tpu_custom_call" | custom-call | tf_op jit(solution)/shard_map/pallas_call | solution.py:244
  94.0 3.3 %copy.11 = f32[24,192,128]{2,1,0:T(8,128)} copy(f32[24,192,128]{2,1,0:T(8,128)} %shard_map.91) | data formatting | bytes 4718592

commit v2 on v1

--- a/solution.py
+++ b/solution.py
@@ -9,6 +9,7 @@
 
 LN_EPS = 1e-5
 LANES = 128
+SEND = 2
 F32, BF16 = jnp.float32, jnp.bfloat16
 
 
@@ -33,7 +34,7 @@
 
 
 def kernel(cfg, z_ref, wqs_ref, wbs_ref, wos_ref, wqe_ref, wbe_ref, woe_ref, w1_ref, w2_ref, out_ref,
-           z1, flat, norm, w_t, w_b, qmask, v_t, gate_t, keys, bias_rows, bias_out, bias_in, bias_t,
+           z1, flat, norm, w_t, w_b, qmask, v_t, gate_t, keys, bias_rows, bias_out, bias_in, bias_t, scores, tops, mixed, upds, normed,
            h_out, h_in, d_out, d_in, out_sem, bias_sem, h_sem, d_sem):
     group, rows, seq, chan, heads, axis = cfg
     dim = chan // heads
@@ -122,41 +123,56 @@
             bias_t[pair, :, pl.ds(LANES, LANES)] = odd[:, :LANES]
             bias_t[2, :, pl.ds(pair * LANES, LANES)] = jnp.where(low, even[:, LANES:], odd[:, LANES:])
 
-    def attention(r, wo):
-        key, qm, vt, gate = keys[r], qmask[r], v_t[r], gate_t[r]
-        zero = jnp.zeros((dim, LANES), BF16)
-        zero2 = jnp.zeros((2 * dim, LANES), BF16)
-        zero4 = jnp.zeros((2 * dim, 2 * LANES), BF16)
-
-        def pair_rhs(pair):
-            a = qm[2 * pair * dim:(2 * pair + 1) * dim, :LANES]
-            b = qm[(2 * pair + 1) * dim:(2 * pair + 2) * dim, :LANES]
-            return jnp.concatenate([jnp.concatenate([a, zero], axis=1), jnp.concatenate([zero, b], axis=1)], axis=0)
-
-        rhs = [jnp.concatenate([pair_rhs(0), zero4], axis=0), jnp.concatenate([zero4, pair_rhs(1)], axis=0),
-               jnp.concatenate([jnp.concatenate([qm[:2 * dim, LANES:], zero2], axis=1),
-                                jnp.concatenate([zero2, qm[2 * dim:, LANES:]], axis=1)], axis=0)]
-        values = [vt[:2 * dim], vt[2 * dim:], vt]
-        mixed = []
-        for t in range(3):
-            s = mm(key, rhs[t]) * scale + bias_t[t]
-            e = jnp.exp(s - jnp.max(s, axis=0, keepdims=True))
-            total = jnp.sum(e, axis=0, keepdims=True)
-            mixed.append(mm(values[t], e.astype(BF16)) * (1.0 / total))
-        main = jnp.concatenate([mixed[0][:dim, :LANES], mixed[0][dim:, LANES:], mixed[1][:dim, :LANES], mixed[1][dim:, LANES:]], axis=0)
-        rest = []
-        for h in range(heads):
-            part = mixed[2][h * dim:(h + 1) * dim, (h // 2) * LANES:(h // 2 + 1) * LANES] * gate[h * dim:(h + 1) * dim, LANES:]
-            rest.append(jnp.where(low if h % 2 == 0 else jnp.logical_not(low), part, 0.0))
-        main = (main * gate[:, :LANES]).astype(BF16)
-        rest = jnp.concatenate(rest, axis=0).astype(BF16)
-        upd = mm(jnp.concatenate([main.T, rest.T], axis=0), wo)
+    zero = jnp.zeros((dim, LANES), BF16)
+    zero2 = jnp.zeros((2 * dim, LANES), BF16)
+    zero4 = jnp.zeros((2 * dim, 2 * LANES), BF16)
+
+    def query_tile(r, t):
+        if t == 2:
+            top = jnp.concatenate([qmask[r, pl.ds(0, 2 * dim), pl.ds(LANES, LANES)], zero2], axis=1)
+            bottom = jnp.concatenate([zero2, qmask[r, pl.ds(2 * dim, 2 * dim), pl.ds(LANES, LANES)]], axis=1)
+            return jnp.concatenate([top, bottom], axis=0)
+        first = qmask[r, pl.ds(2 * t * dim, dim), pl.ds(0, LANES)]
+        second = qmask[r, pl.ds((2 * t + 1) * dim, dim), pl.ds(0, LANES)]
+        pair = jnp.concatenate([jnp.concatenate([first, zero], axis=1), jnp.concatenate([zero, second], axis=1)], axis=0)
+        return jnp.concatenate([pair, zero4] if t == 0 else [zero4, pair], axis=0)
+
+    def score_tile(r, t):
+        s = mm(keys[r], query_tile(r, t)) * scale + bias_t[t]
+        scores[t] = s
+        tops[t] = jnp.max(s, axis=0, keepdims=True)
+
+    def mix_tile(r, t):
+        e = jnp.exp(scores[t] - tops[t])
+        total = jnp.sum(e, axis=0, keepdims=True)
+        values = v_t[r] if t == 2 else v_t[r, pl.ds(2 * t * dim, 2 * dim), :]
+        o = mm(values, e.astype(BF16)) * (1.0 / total)
+        if t < 2:
+            for h in (2 * t, 2 * t + 1):
+                part = o[(h % 2) * dim:(h % 2 + 1) * dim, (h % 2) * LANES:(h % 2 + 1) * LANES]
+                mixed[pl.ds(h * dim, dim), pl.ds(0, LANES)] = (part * gate_t[r, pl.ds(h * dim, dim), pl.ds(0, LANES)]).astype(BF16)
+        else:
+            for h in range(heads):
+                part = o[h * dim:(h + 1) * dim, (h // 2) * LANES:(h // 2 + 1) * LANES] * gate_t[r, pl.ds(h * dim, dim), pl.ds(LANES, LANES)]
+                mixed[pl.ds(h * dim, dim), pl.ds(LANES, LANES)] = jnp.where(low if h % 2 == 0 else jnp.logical_not(low), part, 0.0).astype(BF16)
+
+    def merge_heads(wo):
+        upd = mm(mixed[...].T, wo)
         return jnp.concatenate([upd[:LANES], upd[LANES:LANES + tail] + upd[LANES + tail:]], axis=0)
 
-    def send_row(r, src, dst, sem):
-        mine = pl.ds(me * sub, sub)
-        dst[me, r] = src[r, mine]
-        peers(lambda d: remote(src.at[r, pl.ds(d * sub, sub)], dst.at[me, r], sem, d).start())
+    def pipeline(steps, lag):
+        def step(idx, carry):
+            steps(idx, lambda back: jnp.clip(idx - back, 0, rows - 1))
+            return carry
+
+        lax.fori_loop(0, rows + lag, step, 0)
+
+    def send_rows(last, src, dst, sem):
+        @pl.when(jnp.logical_and(last >= 0, lax.rem(last, SEND) == SEND - 1))
+        def _():
+            some = pl.ds(last - (SEND - 1), SEND)
+            dst[me, some] = src[some, pl.ds(me * sub, sub)]
+            peers(lambda d: remote(src.at[some, pl.ds(d * sub, sub)], dst.at[me, some], sem, d).start())
 
     def unpack(src):
         def part(d):
@@ -169,13 +185,17 @@
     project(wqs_ref)
     spread_bias(0)
 
-    def start_row(r):
-        new = z_ref[r] + attention(r, wos_ref[...])
-        z1[r] = new
-        h_out[r] = new.astype(BF16).reshape(seq // 8, 8, chan)
-        send_row(r, h_out, h_in, h_sem)
-
-    loop(rows, start_row, 2)
+    def start_step(idx, at):
+        r = at(2)
+        z_new = z_ref[r] + merge_heads(wos_ref[...])
+        z1[r] = z_new
+        h_out[r] = z_new.astype(BF16).reshape(seq // 8, 8, chan)
+        for t in range(3):
+            mix_tile(at(1), t)
+            score_tile(at(0), t)
+        send_rows(idx - 2, h_out, h_in, h_sem)
+
+    pipeline(start_step, 2)
 
     load_weights(wqe_ref, wbe_ref)
     wait_recv(h_in, h_sem)
@@ -185,14 +205,18 @@
     project(wqe_ref)
     spread_bias(1)
 
-    def end_row(c):
-        upd = attention(c, woe_ref[...])
-        hidden = jnp.maximum(mm(layer_norm(column(c) + upd), w1_ref[...]), 0.0).astype(BF16)
-        delta = upd + mm(hidden, w2_ref[...])
-        d_out[c] = delta.astype(BF16).reshape(seq // 8, 8, chan)
-        send_row(c, d_out, d_in, d_sem)
-
-    loop(rows, end_row, 2)
+    def end_step(idx, at):
+        hidden = jnp.maximum(mm(normed[...], w1_ref[...]), 0.0).astype(BF16)
+        d_out[at(3)] = (upds[...] + mm(hidden, w2_ref[...])).astype(BF16).reshape(seq // 8, 8, chan)
+        upd = merge_heads(woe_ref[...])
+        upds[...] = upd
+        normed[...] = layer_norm(column(at(2)) + upd)
+        for t in range(3):
+            mix_tile(at(1), t)
+            score_tile(at(0), t)
+        send_rows(idx - 3, d_out, d_in, d_sem)
+
+    pipeline(end_step, 3)
     wait_recv(d_in, d_sem)
     unpack(d_in)
 
@@ -232,6 +256,11 @@
             pltpu.VMEM((2, heads // 2, 3, sub, 8, LANES), BF16),
             pltpu.VMEM((2, group, heads // 2, 3, sub, 8, LANES), BF16),
             pltpu.VMEM((3, seq, packed), F32),
+            pltpu.VMEM((3, seq, packed), F32),
+            pltpu.VMEM((3, 1, packed), F32),
+            pltpu.VMEM((chan, packed), BF16),
+            pltpu.VMEM((seq, chan), F32),
+            pltpu.VMEM((seq, chan), BF16),
             pltpu.VMEM((rows, seq // 8, 8, chan), BF16),
             pltpu.VMEM((group, rows, sub, 8, chan), BF16),
             pltpu.VMEM((rows, seq // 8, 8, chan), BF16),

time: 97.5 us -> 63 us (0.65)
  Pallas kernels: 94 us -> 59.6 us
    pallas_call x1, Pallas kernels: 94 us -> 59.6 us  [local_fn(): pl.pallas_call(functools.partial(kernel, (group, rows, seq, chan, heads,...]
where the time goes in v2:
time: 63 us; the launch traced here: 62.9 us
  Pallas kernels  59.6 us (95%)
  local copies, waits for them, and re-layouts  3.3 us (5%)
    pallas_call x1, Pallas kernels, local_fn(): pl.pallas_call(functools.partial(kernel, (group, rows, seq, chan, heads,...  59.6 us
    unnamed x1, local copies, waits for them, and re-layouts  3.3 us

profile of v2, /device:TPU:81, one launch (start us, length us, event | category | flops | bytes accessed | tf_op | source)
XLA Modules:
  0.0 62.9 jit_solution(637716128703136798)
XLA Ops:
  0.0 59.6 %shard_map.91 = f32[24,192,128]{2,1,0:T(8,128)} custom-call(f32[24,192,128]{2,1,0:T(8,128)} %z_ref.1, bf16[128,512]{1,0:T(8,128)(2,1)} %wqs_ref.1, bf16[4,128]{1,0:T(4,128)(2,1)} %wbs_ref.1, bf16[128,128]{1,0:T(8,128)(2,1)} %wos_ref.1, bf16[128,512]{1,0:T(8,128)(2,1)} %wqe_ref.1, bf16[4,128]{1,0:T(4,128)(2,1)} %wbe_ref.1, bf16[128,128]{1,0:T(8,128)(2,1)} %woe_ref.1, ...), custom_call_target="tpu_custom_call" | custom-call | tf_op jit(solution)/shard_map/pallas_call | solution.py:273
  59.6 3.3 %copy.11 = f32[24,192,128]{2,1,0:T(8,128)} copy(f32[24,192,128]{2,1,0:T(8,128)} %shard_map.91) | data formatting | bytes 4718592

commit v3 on v2

--- a/solution.py
+++ b/solution.py
@@ -33,15 +33,27 @@
     lax.fori_loop(0, count // unroll, step, 0)
 
 
-def kernel(cfg, z_ref, wqs_ref, wbs_ref, wos_ref, wqe_ref, wbe_ref, woe_ref, w1_ref, w2_ref, out_ref,
-           z1, flat, norm, w_t, w_b, qmask, v_t, gate_t, keys, bias_rows, bias_out, bias_in, bias_t, scores, tops, mixed, upds, normed,
-           h_out, h_in, d_out, d_in, out_sem, bias_sem, h_sem, d_sem):
+def kernel(cfg, z_hbm, wqs_hbm, wbs_hbm, wos_hbm, wqe_hbm, wbe_hbm, woe_hbm, w1_hbm, w2_hbm, out_ref,
+           z_ref, wqs_ref, wbs_ref, wos_ref, wqe_ref, wbe_ref, woe_ref, w1_ref, w2_ref,
+           flat, norm, norm_b, w_t, w_b, qmask, v_t, gate_t, keys, bias_rows, bias_out, bias_in, bias_t, scores, tops, mixed, upds, normed,
+           h_out, h_in, d_out, d_in, z_sem, w_sem, out_sem, bias_sem, h_sem, d_sem):
     group, rows, seq, chan, heads, axis = cfg
     dim = chan // heads
     me = lax.axis_index(axis)
     tail = seq - LANES
     sub = rows // 8
     scale = dim ** -0.5
+    early = LANES // group
+
+    loads = []
+    pairs = ((wqs_hbm, wqs_ref), (wbs_hbm, wbs_ref), (wos_hbm, wos_ref), (wqe_hbm, wqe_ref),
+             (wbe_hbm, wbe_ref), (woe_hbm, woe_ref), (w1_hbm, w1_ref), (w2_hbm, w2_ref))
+    z_copy = lambda g: pltpu.make_async_copy(z_hbm.at[pl.ds(g * 8, 8)], z_ref.at[pl.ds(g * 8, 8)], z_sem.at[g])
+    for g in range(sub):
+        z_copy(g).start()
+    for i, (src, dst) in enumerate(pairs):
+        loads.append(pltpu.make_async_copy(src, dst, w_sem.at[i]))
+        loads[i].start()
 
     barrier = pltpu.get_barrier_semaphore()
     for off in range(1, group):
@@ -61,15 +73,15 @@
         return pltpu.make_async_remote_copy(src_ref=src, dst_ref=dst, send_sem=out_sem, recv_sem=recv,
                                             device_id={axis: dst_dev}, device_id_type=pl.DeviceIdType.MESH)
 
-    def wait_recv(ref, sem):
-        part = ref.at[pl.ds(0, group - 1)]
+    def wait_recv(part, sem):
         pltpu.make_async_remote_copy(src_ref=part, dst_ref=part, send_sem=out_sem, recv_sem=sem,
                                      device_id={axis: me}, device_id_type=pl.DeviceIdType.MESH).wait_recv()
 
-    def wait_send(ref):
-        part = ref.at[pl.ds(0, group - 1)]
+    def wait_send(part):
         pltpu.make_async_remote_copy(src_ref=part, dst_ref=part, send_sem=out_sem, recv_sem=out_sem,
                                      device_id={axis: me}, device_id_type=pl.DeviceIdType.MESH).wait_send()
+
+    others = pl.ds(0, group - 1)
 
     def load_weights(wq_ref, wb_ref):
         for dst, src in ((0, 0), (1, 2), (2, 3)):
@@ -77,46 +89,101 @@
         w_b[...] = jnp.zeros(w_b.shape, w_b.dtype)
         w_b[pl.ds(0, heads), :] = wb_ref[...].astype(F32)
 
-    def norm_and_bias(read, phase, first_send):
+    def put_bias(c, tile, even, odd):
+        if tile == 0:
+            for pair in range(heads // 2):
+                bias_rows[pair, 0, pl.ds(c, 1), :] = even[2 * pair:2 * pair + 1]
+                bias_rows[pair, 1, pl.ds(c, 1), :] = even[2 * pair + 1:2 * pair + 2]
+        else:
+            for pair in range(heads // 2):
+                bias_rows[pair, 2, pl.ds(c, 1), :] = jnp.where(low, even[2 * pair:2 * pair + 1], odd[2 * pair + 1:2 * pair + 2])
+
+    def send_bias(phase, tiles, some):
+        rounded = bias_rows[:, tiles, some].astype(BF16).reshape(heads // 2, tiles.size, some.size // 8, 8, LANES)
+        part = pl.ds(some.start // 8, some.size // 8)
+        bias_out[phase, :, tiles, part] = rounded
+        bias_in[phase, me, :, tiles, part] = rounded
+        peers(lambda d: remote(bias_out.at[phase, :, tiles, part], bias_in.at[phase, me, :, tiles, part], bias_sem.at[phase], d).start())
+
+    def start_norm():
         wb = w_b[...].astype(BF16)
-
-        def row(r):
-            u = layer_norm(read(r))
-            norm[r] = u
-            b = mm(wb, doubled(u), ((1,), (1,)))
-            for pair in range(heads // 2):
-                b0, b1 = b[2 * pair:2 * pair + 1], b[2 * pair + 1:2 * pair + 2]
-                bias_rows[pair, 0, pl.ds(r, 1), :] = b0[:, :LANES]
-                bias_rows[pair, 1, pl.ds(r, 1), :] = b1[:, :LANES]
-                bias_rows[pair, 2, pl.ds(r, 1), :] = jnp.where(low, b0[:, LANES:], b1[:, LANES:])
-
-        loop(rows, row, 4)
-        rounded = bias_rows[...].astype(BF16).reshape(bias_out.shape[1:])
-        bias_out[phase] = rounded
-        bias_in[phase, me] = rounded
-        first_send()
-        peers(lambda d: remote(bias_out.at[phase], bias_in.at[phase, me], bias_sem.at[phase], d).start())
-
-    def project(wq_ref):
-        def row(r):
-            u = norm[r]
-            keys[r] = mm(u, wq_ref[:, pl.ds(chan, chan)]).astype(BF16)
-            proj = mm(w_t[...], doubled(u), ((1,), (1,)))
-            q, v, gl = proj[:chan], proj[chan:2 * chan], proj[2 * chan:]
-            qmask[r, :, pl.ds(0, LANES)] = q[:, :LANES].astype(BF16)
+        for g in range(sub):
+            z_copy(g).wait()
+
+            def row(i):
+                r = g * 8 + i
+                u = layer_norm(z_ref[r])
+                norm[r] = u
+                b = mm(wb, doubled(u), ((1,), (1,)))
+                put_bias(r, 0, b[:, :LANES], None)
+                put_bias(r, 1, b[:, LANES:], b[:, LANES:])
+
+            loop(8, row, 4)
+            if g == 0:
+                pl.semaphore_wait(barrier, group - 1)
+            send_bias(0, pl.ds(0, 3), pl.ds(g * 8, 8))
+
+    def put_projected(c, proj, lo, width):
+        q, v, gl = proj[:chan], proj[chan:2 * chan], proj[2 * chan:]
+        v_t[c, :, pl.ds(lo, width)] = v[:, :width].astype(BF16)
+        gate_t[c, :, pl.ds(lo, LANES)] = jax.nn.sigmoid(gl)
+        if lo == 0:
+            qmask[c, :, pl.ds(0, LANES)] = q.astype(BF16)
+        else:
             for h in range(heads):
-                part = q[h * dim:(h + 1) * dim, LANES:]
                 keep = low if h % 2 == 0 else jnp.logical_not(low)
-                qmask[r, pl.ds(h * dim, dim), pl.ds(LANES, LANES)] = jnp.where(keep, part, 0.0).astype(BF16)
-            v_t[r] = v[:, :seq].astype(BF16)
-            gate_t[r] = jax.nn.sigmoid(gl)
-
-        loop(rows, row, 2)
+                qmask[c, pl.ds(h * dim, dim), pl.ds(LANES, LANES)] = jnp.where(keep, q[h * dim:(h + 1) * dim], 0.0).astype(BF16)
+
+    def end_first(i):
+        wb = w_b[...].astype(BF16)
+        u = jnp.concatenate([layer_norm(flat[pl.ds(2 * i + j, LANES, stride=rows), :]) for j in range(2)], axis=0)
+        b = mm(wb, u, ((1,), (1,)))
+        k = mm(u, wqe_ref[:, pl.ds(chan, chan)]).astype(BF16)
+        proj = mm(w_t[...], u, ((1,), (1,)))
+        for j in range(2):
+            cut = slice(j * LANES, (j + 1) * LANES)
+            put_bias(2 * i + j, 0, b[:, cut], None)
+            keys[2 * i + j, pl.ds(0, LANES)] = k[cut]
+            put_projected(2 * i + j, proj[:, cut], 0, LANES)
+
+    def end_second(i):
+        wb = w_b[...].astype(BF16)
+        u = [layer_norm(flat[pl.ds(LANES * rows + 2 * i + j, tail, stride=rows), :]) for j in range(2)]
+        u = jnp.concatenate([u[0], u[0], u[1], u[1]], axis=0)
+        norm_b[i] = u
+        b = mm(wb, u, ((1,), (1,)))
+        for j in range(2):
+            cut = slice(j * LANES, (j + 1) * LANES)
+            put_bias(2 * i + j, 1, b[:, cut], b[:, cut])
+
+    def end_third(i):
+        u = norm_b[i]
+        k = mm(jnp.concatenate([u[:tail], u[LANES:LANES + tail]], axis=0), wqe_ref[:, pl.ds(chan, chan)]).astype(BF16)
+        proj = mm(w_t[...], u, ((1,), (1,)))
+        for j in range(2):
+            keys[2 * i + j, pl.ds(LANES, tail)] = k[j * tail:(j + 1) * tail]
+            put_projected(2 * i + j, proj[:, j * LANES:(j + 1) * LANES], LANES, tail)
+
+    def start_project(r):
+        u = norm[r]
+        keys[r] = mm(u, wqs_ref[:, pl.ds(chan, chan)]).astype(BF16)
+        proj = mm(w_t[...], doubled(u), ((1,), (1,)))
+        put_projected(r, proj[:, :LANES], 0, LANES)
+        put_projected(r, proj[:, LANES:], LANES, tail)
 
     def spread_bias(phase):
-        wait_recv(bias_in.at[phase], bias_sem.at[phase])
+        wait_recv(bias_in.at[phase, others], bias_sem.at[phase])
         for pair in range(heads // 2):
-            t0, t1, t2 = [doubled(bias_in[phase, :, pair, t].astype(F32).reshape(group * rows, LANES)).T for t in range(3)]
+            tiles = []
+            for t in range(3):
+                b = bias_in[phase, :, pair, t].astype(F32)
+                if phase == 0:
+                    b = doubled(b.reshape(seq, LANES))
+                else:
+                    late = b[:, early // 8:].reshape(tail, LANES)
+                    b = jnp.concatenate([b[:, :early // 8].reshape(LANES, LANES), late, late], axis=0)
+                tiles.append(b.T)
+            t0, t1, t2 = tiles
             even = jnp.concatenate([t0, t2[:tail]], axis=0)
             odd = jnp.concatenate([t1, t2[tail:]], axis=0)
             bias_t[pair, :, pl.ds(0, LANES)] = even[:, :LANES]
@@ -170,65 +237,83 @@
     def send_rows(last, src, dst, sem):
         @pl.when(jnp.logical_and(last >= 0, lax.rem(last, SEND) == SEND - 1))
         def _():
-            some = pl.ds(last - (SEND - 1), SEND)
+            first = last - (SEND - 1)
+            some = pl.ds(first, SEND)
             dst[me, some] = src[some, pl.ds(me * sub, sub)]
-            peers(lambda d: remote(src.at[some, pl.ds(d * sub, sub)], dst.at[me, some], sem, d).start())
-
-    def unpack(src):
+            peers(lambda d: remote(src.at[some, pl.ds(d * sub, sub)], dst.at[me, some], sem(first), d).start())
+
+    def unpack(src, lo, count, base):
         def part(d):
-            flat[pl.ds(d * rows * rows, rows * rows), :] = src[d].astype(F32).reshape(rows * rows, chan)
+            flat[pl.ds(base + d * count * rows, count * rows), :] = src[d, pl.ds(lo, count)].astype(F32).reshape(count * rows, chan)
 
         loop(group, part)
 
+    loads[0].wait()
+    loads[1].wait()
     load_weights(wqs_ref, wbs_ref)
-    norm_and_bias(lambda r: z_ref[r], 0, lambda: pl.semaphore_wait(barrier, group - 1))
-    project(wqs_ref)
+    start_norm()
+    loop(rows, start_project, 2)
+    for load in loads[2:]:
+        load.wait()
     spread_bias(0)
 
     def start_step(idx, at):
         r = at(2)
         z_new = z_ref[r] + merge_heads(wos_ref[...])
-        z1[r] = z_new
+        out_ref[r] = z_new
         h_out[r] = z_new.astype(BF16).reshape(seq // 8, 8, chan)
         for t in range(3):
             mix_tile(at(1), t)
             score_tile(at(0), t)
-        send_rows(idx - 2, h_out, h_in, h_sem)
+        send_rows(idx - 2, h_out, h_in, lambda first: h_sem.at[first // early])
 
     pipeline(start_step, 2)
 
     load_weights(wqe_ref, wbe_ref)
-    wait_recv(h_in, h_sem)
-    unpack(h_in)
+    wait_recv(h_in.at[others, pl.ds(0, early)], h_sem.at[0])
+    unpack(h_in, 0, early, 0)
+    loop(rows // 2, end_first)
+    send_bias(1, pl.ds(0, 2), pl.ds(0, rows))
+    wait_recv(h_in.at[others, pl.ds(early, rows - early)], h_sem.at[1])
+    unpack(h_in, early, rows - early, LANES * rows)
+    loop(rows // 2, end_second, 2)
+    send_bias(1, pl.ds(2, 1), pl.ds(0, rows))
+    loop(rows // 2, end_third)
+    spread_bias(1)
     column = lambda c: flat[pl.ds(c, seq, stride=rows), :]
-    norm_and_bias(column, 1, lambda: None)
-    project(wqe_ref)
-    spread_bias(1)
+
+    def by_owner(vals):
+        parts = vals.reshape(seq // 8, 8, chan)
+        base = LANES // 8
+        order = []
+        for d in range(group):
+            order.append(parts[d * early // 8:(d + 1) * early // 8])
+            order.append(parts[base + d * (sub - early // 8):base + (d + 1) * (sub - early // 8)])
+        return jnp.concatenate(order, axis=0)
 
     def end_step(idx, at):
         hidden = jnp.maximum(mm(normed[...], w1_ref[...]), 0.0).astype(BF16)
-        d_out[at(3)] = (upds[...] + mm(hidden, w2_ref[...])).astype(BF16).reshape(seq // 8, 8, chan)
+        d_out[at(3)] = by_owner(upds[...] + mm(hidden, w2_ref[...])).astype(BF16)
         upd = merge_heads(woe_ref[...])
         upds[...] = upd
         normed[...] = layer_norm(column(at(2)) + upd)
         for t in range(3):
             mix_tile(at(1), t)
             score_tile(at(0), t)
-        send_rows(idx - 3, d_out, d_in, d_sem)
+        send_rows(idx - 3, d_out, d_in, lambda first: d_sem)
 
     pipeline(end_step, 3)
-    wait_recv(d_in, d_sem)
-    unpack(d_in)
+    wait_recv(d_in.at[others], d_sem)
+    unpack(d_in, 0, rows, 0)
 
     def final(r):
-        out_ref[r] = z1[r] + flat[pl.ds(r, seq, stride=rows), :]
+        out_ref[r] = out_ref[r] + flat[pl.ds(r, seq, stride=rows), :]
 
     loop(rows, final, 2)
     for phase in range(2):
-        for _ in range(group - 1):
-            remote(bias_out.at[phase], bias_in.at[phase, me], bias_sem.at[phase], me).wait_send()
-    wait_send(h_in)
-    wait_send(d_in)
+        wait_send(bias_in.at[phase, others])
+    wait_send(h_in.at[others])
+    wait_send(d_in.at[others])
 
 
 def solution(mesh):
@@ -241,11 +326,11 @@
         heads = w_bias_s.shape[0]
         sub = rows // 8
         packed = 2 * LANES
-        vmem = pl.BlockSpec(memory_space=pltpu.VMEM)
-        scratch = [
-            pltpu.VMEM((rows, seq, chan), F32),
+        weights = (w_qkvg_s, w_bias_s, w_out_s, w_qkvg_e, w_bias_e, w_out_e, w_one, w_two)
+        scratch = [pltpu.VMEM(pair_loc.shape, F32)] + [pltpu.VMEM(w.shape, w.dtype) for w in weights] + [
             pltpu.VMEM((rows * seq, chan), F32),
             pltpu.VMEM((rows, seq, chan), BF16),
+            pltpu.VMEM((rows // 2, packed, chan), BF16),
             pltpu.VMEM((3 * chan, chan), BF16),
             pltpu.VMEM((16, chan), F32),
             pltpu.VMEM((rows, chan, packed), BF16),
@@ -265,18 +350,20 @@
             pltpu.VMEM((group, rows, sub, 8, chan), BF16),
             pltpu.VMEM((rows, seq // 8, 8, chan), BF16),
             pltpu.VMEM((group, rows, sub, 8, chan), BF16),
+            pltpu.SemaphoreType.DMA((sub,)),
+            pltpu.SemaphoreType.DMA((len(weights),)),
             pltpu.SemaphoreType.DMA,
             pltpu.SemaphoreType.DMA((2,)),
-            pltpu.SemaphoreType.DMA,
+            pltpu.SemaphoreType.DMA((2,)),
             pltpu.SemaphoreType.DMA,
         ]
         return pl.pallas_call(
             functools.partial(kernel, (group, rows, seq, chan, heads, axis)),
             out_shape=jax.ShapeDtypeStruct(pair_loc.shape, F32),
-            in_specs=[vmem] * 9,
-            out_specs=vmem,
+            in_specs=[pl.BlockSpec(memory_space=pltpu.HBM)] * 9,
+            out_specs=pl.BlockSpec(memory_space=pltpu.VMEM),
             scratch_shapes=scratch,
-            compiler_params=pltpu.CompilerParams(collective_id=0, has_side_effects=True, vmem_limit_bytes=60 * 2 ** 20),
-        )(pair_loc, w_qkvg_s, w_bias_s, w_out_s, w_qkvg_e, w_bias_e, w_out_e, w_one, w_two)
+            compiler_params=pltpu.CompilerParams(collective_id=0, has_side_effects=True, vmem_limit_bytes=40 * 2 ** 20),
+        )(*[pltpu.with_memory_space_constraint(x, pltpu.HBM) for x in (pair_loc, *weights)])
 
     return jax.shard_map(local_fn, mesh=mesh, in_specs=(row_spec, P(), P(), P(), P(), P(), P(), P(), P()), out_specs=row_spec, check_vma=False)

time: 63 us -> 56.6 us (0.90)
  Pallas kernels: 59.6 us -> 55 us
  local copies, waits for them, and re-layouts: 3.3 us -> 1.41 us
    pallas_call x1, Pallas kernels: 59.6 us -> 55 us  [local_fn(): pl.pallas_call(functools.partial(kernel, (group, rows, seq, chan, heads,...]
    unnamed x1, local copies, waits for them, and re-layouts: 3.3 us -> 1.41 us
where the time goes in v3:
time: 56.6 us; the launch traced here: 56.5 us
  Pallas kernels  55 us (97%)
  local copies, waits for them, and re-layouts  1.41 us (2%)
    pallas_call x1, Pallas kernels, local_fn(): pl.pallas_call(functools.partial(kernel, (group, rows, seq, chan, heads,...  55 us
    unnamed x1, local copies, waits for them, and re-layouts  1.41 us

profile of v3, /device:TPU:81, one launch (start us, length us, event | category | flops | bytes accessed | tf_op | source)
XLA Modules:
  0.0 56.5 jit_solution(758393418751002957)
XLA Ops:
  0.0 55.0 %shard_map.91 = f32[24,192,128]{2,1,0:T(8,128)S(1)} custom-call(f32[24,192,128]{2,1,0:T(8,128)} %z_hbm.1, bf16[128,512]{1,0:T(8,128)(2,1)} %wqs_hbm.1, bf16[4,128]{1,0:T(4,128)(2,1)} %wbs_hbm.1, bf16[128,128]{1,0:T(8,128)(2,1)} %wos_hbm.1, bf16[128,512]{1,0:T(8,128)(2,1)} %wqe_hbm.1, bf16[4,128]{1,0:T(4,128)(2,1)} %wbe_hbm.1, bf16[128,128]{1,0:T(8,128)(2,1)} %woe_hbm.1, ...), custom_call_target="tpu_custom_call" | custom-call | tf_op jit(solution)/shard_map/pallas_call | solution.py:360
  55.0 1.4 %copy.11 = f32[24,192,128]{2,1,0:T(8,128)} copy(f32[24,192,128]{2,1,0:T(8,128)S(1)} %shard_map.91) | data formatting | bytes 4718592

commit v4 on v3

v4 whole, which is shorter than its diff:
```python
import functools

import jax
import jax.numpy as jnp
from jax import lax
from jax.experimental import pallas as pl
from jax.experimental.pallas import tpu as pltpu
from jax.sharding import PartitionSpec as P

LN_EPS = 1e-5
LANES = 128
SEND = 2
F32, BF16 = jnp.float32, jnp.bfloat16


def layer_norm(vals):
    mean = jnp.mean(vals, axis=-1, keepdims=True)
    centered = vals - mean
    var = jnp.mean(centered * centered, axis=-1, keepdims=True)
    return (centered * lax.rsqrt(var + LN_EPS)).astype(BF16)


def mm(lhs, rhs, contract=((1,), (0,))):
    return lax.dot_general(lhs, rhs, (contract, ((), ())), preferred_element_type=F32)


def loop(count, body, unroll=1):
    def step(idx, carry):
        for sub in range(unroll):
            body(idx * unroll + sub)
        return carry

    lax.fori_loop(0, count // unroll, step, 0)


def kernel(cfg, z_hbm, wqs_hbm, wbs_hbm, wos_hbm, wqe_hbm, wbe_hbm, woe_hbm, w1_hbm, w2_hbm, out_ref,
           z_ref, wqs_ref, wbs_ref, wos_ref, wqe_ref, wbe_ref, woe_ref, w1_ref, w2_ref,
           flat, norm, w_b, qmask, v_t, gate, keys, bias_rows, bias_out, bias_in, bias_t, scores, tops, mixed, upds, normed,
           h_out, h_in, d_out, d_in, z_sem, w_sem, out_sem, start_sem, far_sem, near_sem, h_sem, d_sem):
    group, rows, seq, chan, heads, axis = cfg
    dim = chan // heads
    me = lax.axis_index(axis)
    tail = seq - LANES
    sub = rows // 8
    scale = dim ** -0.5
    early = LANES // group

    loads = []
    pairs = ((wqs_hbm, wqs_ref), (wbs_hbm, wbs_ref), (wos_hbm, wos_ref), (wqe_hbm, wqe_ref),
             (wbe_hbm, wbe_ref), (woe_hbm, woe_ref), (w1_hbm, w1_ref), (w2_hbm, w2_ref))
    z_copy = lambda g: pltpu.make_async_copy(z_hbm.at[pl.ds(g * 8, 8)], z_ref.at[pl.ds(g * 8, 8)], z_sem.at[g])
    for g in range(sub):
        z_copy(g).start()
    for i, (src, dst) in enumerate(pairs):
        loads.append(pltpu.make_async_copy(src, dst, w_sem.at[i]))
        loads[i].start()

    barrier = pltpu.get_barrier_semaphore()
    for off in range(1, group):
        pl.semaphore_signal(barrier, inc=1, device_id={axis: lax.rem(me + off, group)}, device_id_type=pl.DeviceIdType.MESH)

    lane = lax.broadcasted_iota(jnp.int32, (1, LANES), 1)
    low = lane < tail
    even_head = (lane // dim) % 2 == 0

    def doubled(rows_in):
        return jnp.concatenate([rows_in, rows_in[LANES:seq]], axis=0)

    def peers(start):
        for off in range(1, group):
            start(lax.rem(me + off, group))

    def remote(src, dst, recv, dst_dev):
        return pltpu.make_async_remote_copy(src_ref=src, dst_ref=dst, send_sem=out_sem, recv_sem=recv,
                                            device_id={axis: dst_dev}, device_id_type=pl.DeviceIdType.MESH)

    def wait_recv(part, sem):
        pltpu.make_async_remote_copy(src_ref=part, dst_ref=part, send_sem=out_sem, recv_sem=sem,
                                     device_id={axis: me}, device_id_type=pl.DeviceIdType.MESH).wait_recv()

    def wait_send(part):
        pltpu.make_async_remote_copy(src_ref=part, dst_ref=part, send_sem=out_sem, recv_sem=out_sem,
                                     device_id={axis: me}, device_id_type=pl.DeviceIdType.MESH).wait_send()

    others = pl.ds(0, group - 1)

    def load_bias_weight(phase, wb_ref):
        w_b[phase] = jnp.zeros(w_b.shape[1:], w_b.dtype)
        w_b[phase, pl.ds(0, heads), :] = wb_ref[...].astype(F32)

    def put_bias(r, wb, u):
        b = mm(wb, doubled(u), ((1,), (1,)))
        for pair in range(heads // 2):
            even, odd = b[2 * pair:2 * pair + 1], b[2 * pair + 1:2 * pair + 2]
            bias_rows[pair, 0, pl.ds(r, 1), :] = even[:, :LANES]
            bias_rows[pair, 1, pl.ds(r, 1), :] = odd[:, :LANES]
            bias_rows[pair, 2, pl.ds(r, 1), :] = jnp.where(low, even[:, LANES:], odd[:, LANES:])

    def round_bias(phase, g):
        rounded = bias_rows[:, :, pl.ds(pl.multiple_of(g * 8, 8), 8)].astype(BF16).reshape(heads // 2, 3, 1, 8, LANES)
        bias_out[phase, :, :, pl.ds(g, 1)] = rounded
        bias_in[phase, me, :, :, pl.ds(g, 1)] = rounded

    def bias_copy(phase, g, src, slot, sem, d):
        return remote(src, bias_in.at[phase, slot, :, :, pl.ds(g, 1)], sem, d)

    def send_start_bias(g):
        round_bias(0, g)
        src = bias_out.at[0, :, :, pl.ds(g, 1)]
        peers(lambda d: bias_copy(0, g, src, me, start_sem, d).start())

    twin = me + 1 - 2 * lax.rem(me, 2)

    def send_end_bias(g):
        round_bias(1, g)
        src = bias_out.at[1, :, :, pl.ds(g, 1)]
        for off in range(2, group, 2):
            bias_copy(1, g, src, me, far_sem.at[g], lax.rem(me + off, group)).start()
        bias_copy(1, g, src, me, near_sem, twin).start()

    def relay_bias(g):
        wait_recv(bias_in.at[1, pl.ds(0, group // 2 - 1), :, :, pl.ds(g, 1)], far_sem.at[g])
        for off in range(2, group, 2):
            slot = lax.rem(me + off, group)
            bias_copy(1, g, bias_in.at[1, slot, :, :, pl.ds(g, 1)], slot, near_sem, twin).start()

    def start_norm():
        wb = w_b[0].astype(BF16)
        for g in range(sub):
            z_copy(g).wait()

            def row(i):
                r = g * 8 + i
                u = layer_norm(z_ref[r])
                norm[r] = u
                put_bias(r, wb, u)

            loop(8, row, 4)
            if g == 0:
                pl.semaphore_wait(barrier, group - 1)
            send_start_bias(g)

    def project(c, u, lo, width, wq):
        y = mm(u, wq)
        q, k, v, gl = [y[:, i * chan:(i + 1) * chan] for i in range(4)]
        keys[c, pl.ds(lo, width)] = k.astype(BF16)
        gate[c, pl.ds(lo, width)] = jax.nn.sigmoid(gl)
        late = q[width - tail:]
        masked = [jnp.where(even_head, late, 0.0), jnp.where(even_head, 0.0, late)]
        twice = [v[width - tail:], v[width - tail:]]
        if lo == 0:
            qmask[c, :, pl.ds(0, LANES)] = q[:LANES].astype(BF16).T
            v_t[c, :, pl.ds(0, LANES)] = v[:LANES].astype(BF16).T
        if lo + width == seq:
            qmask[c, :, pl.ds(LANES, LANES)] = jnp.concatenate(masked, axis=0).astype(BF16).T
            v_t[c, :, pl.ds(LANES, LANES)] = jnp.concatenate(twice, axis=0).astype(BF16).T

    def spread_start_bias():
        wait_recv(bias_in.at[0, others], start_sem)
        for pair in range(heads // 2):
            t0, t1, t2 = [doubled(bias_in[0, :, pair, t].astype(F32).reshape(seq, LANES)).T for t in range(3)]
            even = jnp.concatenate([t0, t2[:tail]], axis=0)
            odd = jnp.concatenate([t1, t2[tail:]], axis=0)
            bias_t[pair, :, pl.ds(0, LANES)] = even[:, :LANES]
            bias_t[pair, :, pl.ds(LANES, LANES)] = odd[:, :LANES]
            bias_t[2, :, pl.ds(pair * LANES, LANES)] = jnp.where(low, even[:, LANES:], odd[:, LANES:])

    def spread_end_bias():
        wait_recv(bias_in.at[1, pl.ds(0, group // 2)], near_sem)
        for pair in range(heads // 2):
            for t in range(3):
                b = bias_in[1, :, pair, t].astype(F32)
                b = jnp.concatenate([b[:, :early // 8].reshape(LANES, LANES), b[:, early // 8:].reshape(tail, LANES)], axis=0)
                if t < 2:
                    bias_t[pair, :, pl.ds(t * LANES, LANES)] = b
                else:
                    bias_t[2, :, pl.ds(pair * LANES, LANES)] = b

    zero = jnp.zeros((dim, LANES), BF16)
    zero2 = jnp.zeros((2 * dim, LANES), BF16)
    zero4 = jnp.zeros((2 * dim, 2 * LANES), BF16)

    def query_tile(r, t):
        if t == 2:
            top = jnp.concatenate([qmask[r, pl.ds(0, 2 * dim), pl.ds(LANES, LANES)], zero2], axis=1)
            bottom = jnp.concatenate([zero2, qmask[r, pl.ds(2 * dim, 2 * dim), pl.ds(LANES, LANES)]], axis=1)
            return jnp.concatenate([top, bottom], axis=0)
        first = qmask[r, pl.ds(2 * t * dim, dim), pl.ds(0, LANES)]
        second = qmask[r, pl.ds((2 * t + 1) * dim, dim), pl.ds(0, LANES)]
        pair = jnp.concatenate([jnp.concatenate([first, zero], axis=1), jnp.concatenate([zero, second], axis=1)], axis=0)
        return jnp.concatenate([pair, zero4] if t == 0 else [zero4, pair], axis=0)

    def score_tile(r, slot, t):
        s = mm(keys[r], query_tile(r, t)) * scale + bias_t[t]
        scores[slot, t] = s
        tops[slot, t] = jnp.max(s, axis=0, keepdims=True)

    def mix_tile(r, slot, t):
        e = jnp.exp(scores[slot, t] - tops[slot, t])
        total = jnp.sum(e, axis=0, keepdims=True)
        values = v_t[r, :, pl.ds(0, seq)] if t == 2 else v_t[r, pl.ds(2 * t * dim, 2 * dim), pl.ds(0, seq)]
        o = mm(values, e.astype(BF16)) * (1.0 / total)
        if t < 2:
            for h in (2 * t, 2 * t + 1):
                mixed[slot, pl.ds(h * dim, dim), pl.ds(0, LANES)] = o[(h % 2) * dim:(h % 2 + 1) * dim, (h % 2) * LANES:(h % 2 + 1) * LANES]
        else:
            for h in range(heads):
                mixed[slot, pl.ds(h * dim, dim), pl.ds(LANES, LANES)] = o[h * dim:(h + 1) * dim, (h // 2) * LANES:(h // 2 + 1) * LANES]

    def merge_heads(r, slot, wo):
        o = mixed[slot].T
        o = jnp.concatenate([o[:LANES], jnp.where(even_head, o[LANES:LANES + tail], o[LANES + tail:])], axis=0)
        return mm((o * gate[r]).astype(BF16), wo)

    def pipeline(stages, send):
        depth, count = len(stages), rows // 2

        def turn(i, active):
            for stage in sorted(active, reverse=True):
                for slot in range(2):
                    stages[stage](2 * (i - stage) + slot, slot)
            send(i, active)

        for i in range(depth - 1):
            turn(i, range(i + 1))

        def step(i, carry):
            turn(i, range(depth))
            return carry

        lax.fori_loop(depth - 1, count, step, 0)
        for i in range(count, count + depth - 1):
            turn(i, range(i - count + 1, depth))

    def score(r, slot):
        for t in range(3):
            score_tile(r, slot, t)

    def mix(r, slot):
        for t in range(3):
            mix_tile(r, slot, t)

    def send_rows(first, src, dst, sem):
        some = pl.ds(first, SEND)
        dst[me, some] = src[some, pl.ds(me * sub, sub)]
        peers(lambda d: remote(src.at[some, pl.ds(d * sub, sub)], dst.at[me, some], sem(first), d).start())

    def unpack(src, lo, count, base):
        def part(d):
            flat[pl.ds(base + d * count * rows, count * rows), :] = src[d, pl.ds(lo, count)].astype(F32).reshape(count * rows, chan)

        loop(group, part)

    def by_place(vals):
        parts = vals.reshape(group, sub, 8, chan)
        return jnp.concatenate([parts[:, :early // 8].reshape(LANES, chan), parts[:, early // 8:].reshape(tail, chan)], axis=0)

    loads[1].wait()
    load_bias_weight(0, wbs_ref)
    start_norm()
    loads[0].wait()
    loop(rows, lambda r: project(r, norm[r], 0, seq, wqs_ref[...]), 2)
    for load in loads[2:]:
        load.wait()
    load_bias_weight(1, wbe_ref)
    spread_start_bias()

    def start_merge(r, slot):
        z_new = z_ref[r] + merge_heads(r, slot, wos_ref[...])
        out_ref[r] = z_new
        h_out[r] = z_new.astype(BF16).reshape(seq // 8, 8, chan)

    def end_bias(r, slot):
        h = out_ref[r].astype(BF16).astype(F32)
        put_bias(r, w_b[1].astype(BF16), layer_norm(by_place(h)))

    def start_send(i, active):
        if 2 in active:
            send_rows(2 * (i - 2), h_out, h_in, lambda r: h_sem.at[r // early])
        if 3 in active:
            r = 2 * (i - 3)
            if isinstance(r, int):
                if r % 8 == 6:
                    send_end_bias(r // 8)
            else:
                @pl.when(lax.rem(r, 8) == 6)
                def _():
                    send_end_bias(r // 8)

    pipeline((score, mix, start_merge, end_bias), start_send)

    for g in range(sub - 1):
        relay_bias(g)
    wait_recv(h_in.at[others, pl.ds(0, early)], h_sem.at[0])
    unpack(h_in, 0, early, 0)

    def end_project(lo, width):
        return lambda c: project(c, layer_norm(flat[pl.ds(lo * rows + c, width, stride=rows), :]), lo, width, wqe_ref[...])

    loop(rows, end_project(0, LANES), 2)
    wait_recv(h_in.at[others, pl.ds(early, rows - early)], h_sem.at[1])
    relay_bias(sub - 1)
    unpack(h_in, early, rows - early, LANES * rows)
    loop(rows, end_project(LANES, tail), 4)
    spread_end_bias()
    column = lambda c: flat[pl.ds(c, seq, stride=rows), :]

    def by_owner(vals):
        parts = vals.reshape(seq // 8, 8, chan)
        base = LANES // 8
        order = []
        for d in range(group):
            order.append(parts[d * early // 8:(d + 1) * early // 8])
            order.append(parts[base + d * (sub - early // 8):base + (d + 1) * (sub - early // 8)])
        return jnp.concatenate(order, axis=0)

    def end_merge(c, slot):
        upd = merge_heads(c, slot, woe_ref[...])
        upds[slot] = upd
        normed[slot] = layer_norm(column(c) + upd)

    def transition(c, slot):
        hidden = jnp.maximum(mm(normed[slot], w1_ref[...]), 0.0).astype(BF16)
        d_out[c] = by_owner(upds[slot] + mm(hidden, w2_ref[...])).astype(BF16)

    def end_send(i, active):
        if 3 in active:
            send_rows(2 * (i - 3), d_out, d_in, lambda c: d_sem.at[c // 8])

    pipeline((score, mix, end_merge, transition), end_send)
    for g in range(sub):
        wait_recv(d_in.at[others, pl.ds(g * 8, 8)], d_sem.at[g])

        def part(d):
            flat[pl.ds((d * rows + g * 8) * rows, 8 * rows), :] = d_in[d, pl.ds(g * 8, 8)].astype(F32).reshape(8 * rows, chan)

        loop(group, part, 2)

        def final(r):
            for d in range(group):
                at = d * rows + g * 8
                out_ref[r, pl.ds(at, 8), :] = out_ref[r, pl.ds(at, 8), :] + flat[pl.ds(at * rows + r, 8, stride=rows), :]

        loop(rows, final, 4)

    for phase in range(2):
        wait_send(bias_in.at[phase, others])
    wait_send(h_in.at[others])
    wait_send(d_in.at[others])


def solution(mesh):
    axis = 'sp'
    group = mesh.shape[axis]
    row_spec = P(('dp', 'sp'), None, None)

    def local_fn(pair_loc, w_qkvg_s, w_bias_s, w_out_s, w_qkvg_e, w_bias_e, w_out_e, w_one, w_two):
        rows, seq, chan = pair_loc.shape
        heads = w_bias_s.shape[0]
        sub = rows // 8
        packed = 2 * LANES
        weights = (w_qkvg_s, w_bias_s, w_out_s, w_qkvg_e, w_bias_e, w_out_e, w_one, w_two)
        scratch = [pltpu.VMEM(pair_loc.shape, F32)] + [pltpu.VMEM(w.shape, w.dtype) for w in weights] + [
            pltpu.VMEM((rows * seq, chan), F32),
            pltpu.VMEM((rows, seq, chan), BF16),
            pltpu.VMEM((2, 16, chan), F32),
            pltpu.VMEM((rows, chan, packed), BF16),
            pltpu.VMEM((rows, chan, packed), BF16),
            pltpu.VMEM((rows, seq, chan), F32),
            pltpu.VMEM((rows, seq, chan), BF16),
            pltpu.VMEM((heads // 2, 3, rows, LANES), F32),
            pltpu.VMEM((2, heads // 2, 3, sub, 8, LANES), BF16),
            pltpu.VMEM((2, group, heads // 2, 3, sub, 8, LANES), BF16),
            pltpu.VMEM((3, seq, packed), F32),
            pltpu.VMEM((2, 3, seq, packed), F32),
            pltpu.VMEM((2, 3, 1, packed), F32),
            pltpu.VMEM((2, chan, packed), F32),
            pltpu.VMEM((2, seq, chan), F32),
            pltpu.VMEM((2, seq, chan), BF16),
            pltpu.VMEM((rows, seq // 8, 8, chan), BF16),
            pltpu.VMEM((group, rows, sub, 8, chan), BF16),
            pltpu.VMEM((rows, seq // 8, 8, chan), BF16),
            pltpu.VMEM((group, rows, sub, 8, chan), BF16),
            pltpu.SemaphoreType.DMA((sub,)),
            pltpu.SemaphoreType.DMA((len(weights),)),
            pltpu.SemaphoreType.DMA,
            pltpu.SemaphoreType.DMA,
            pltpu.SemaphoreType.DMA((sub,)),
            pltpu.SemaphoreType.DMA,
            pltpu.SemaphoreType.DMA((2,)),
            pltpu.SemaphoreType.DMA((sub,)),
        ]
        return pl.pallas_call(
            functools.partial(kernel, (group, rows, seq, chan, heads, axis)),
            out_shape=jax.ShapeDtypeStruct(pair_loc.shape, F32),
            in_specs=[pl.BlockSpec(memory_space=pltpu.HBM)] * 9,
            out_specs=pl.BlockSpec(memory_space=pltpu.VMEM),
            scratch_shapes=scratch,
            compiler_params=pltpu.CompilerParams(collective_id=0, has_side_effects=True, vmem_limit_bytes=40 * 2 ** 20),
        )(*[pltpu.with_memory_space_constraint(x, pltpu.HBM) for x in (pair_loc, *weights)])

    return jax.shard_map(local_fn, mesh=mesh, in_specs=(row_spec, P(), P(), P(), P(), P(), P(), P(), P()), out_specs=row_spec, check_vma=False)
```

time: 56.6 us -> 53.5 us (0.945)
  Pallas kernels: 55 us -> 52 us
    pallas_call x1, Pallas kernels: 55 us -> 52 us  [local_fn(): pl.pallas_call(functools.partial(kernel, (group, rows, seq, chan, heads,...]
where the time goes in v4:
time: 53.5 us; the launch traced here: 53.4 us
  Pallas kernels  52 us (97%)
  local copies, waits for them, and re-layouts  1.41 us (3%)
    pallas_call x1, Pallas kernels, local_fn(): pl.pallas_call(functools.partial(kernel, (group, rows, seq, chan, heads,...  52 us
    unnamed x1, local copies, waits for them, and re-layouts  1.41 us

profile of v4, /device:TPU:81, one launch (start us, length us, event | category | flops | bytes accessed | tf_op | source)
XLA Modules:
  0.0 53.4 jit_solution(13402738950634567750)
XLA Ops:
  0.0 52.0 %shard_map.91 = f32[24,192,128]{2,1,0:T(8,128)S(1)} custom-call(f32[24,192,128]{2,1,0:T(8,128)} %z_hbm.1, bf16[128,512]{1,0:T(8,128)(2,1)} %wqs_hbm.1, bf16[4,128]{1,0:T(4,128)(2,1)} %wbs_hbm.1, bf16[128,128]{1,0:T(8,128)(2,1)} %wos_hbm.1, bf16[128,512]{1,0:T(8,128)(2,1)} %wqe_hbm.1, bf16[4,128]{1,0:T(4,128)(2,1)} %wbe_hbm.1, bf16[128,128]{1,0:T(8,128)(2,1)} %woe_hbm.1, ...), custom_call_target="tpu_custom_call" | custom-call | tf_op jit(solution)/shard_map/pallas_call | solution.py:393
  52.0 1.4 %copy.11 = f32[24,192,128]{2,1,0:T(8,128)} copy(f32[24,192,128]{2,1,0:T(8,128)S(1)} %shard_map.91) | data formatting | bytes 4718592

commit v5 on v4

--- a/solution.py
+++ b/solution.py
@@ -36,7 +36,7 @@
 def kernel(cfg, z_hbm, wqs_hbm, wbs_hbm, wos_hbm, wqe_hbm, wbe_hbm, woe_hbm, w1_hbm, w2_hbm, out_ref,
            z_ref, wqs_ref, wbs_ref, wos_ref, wqe_ref, wbe_ref, woe_ref, w1_ref, w2_ref,
            flat, norm, w_b, qmask, v_t, gate, keys, bias_rows, bias_out, bias_in, bias_t, scores, tops, mixed, upds, normed,
-           h_out, h_in, d_out, d_in, z_sem, w_sem, out_sem, start_sem, far_sem, near_sem, h_sem, d_sem):
+           h_out, h_in, d_out, d_in, z_sem, w_sem, out_sem, far_sem, near_sem, h_sem, d_sem):
     group, rows, seq, chan, heads, axis = cfg
     dim = chan // heads
     me = lax.axis_index(axis)
@@ -53,7 +53,7 @@
         z_copy(g).start()
     for i, (src, dst) in enumerate(pairs):
         loads.append(pltpu.make_async_copy(src, dst, w_sem.at[i]))
-        loads[i].start()
+    loads[1].start()
 
     barrier = pltpu.get_barrier_semaphore()
     for off in range(1, group):
@@ -101,28 +101,31 @@
         bias_out[phase, :, :, pl.ds(g, 1)] = rounded
         bias_in[phase, me, :, :, pl.ds(g, 1)] = rounded
 
+    twin = me + 1 - 2 * lax.rem(me, 2)
+
     def bias_copy(phase, g, src, slot, sem, d):
-        return remote(src, bias_in.at[phase, slot, :, :, pl.ds(g, 1)], sem, d)
-
-    def send_start_bias(g):
-        round_bias(0, g)
-        src = bias_out.at[0, :, :, pl.ds(g, 1)]
-        peers(lambda d: bias_copy(0, g, src, me, start_sem, d).start())
-
-    twin = me + 1 - 2 * lax.rem(me, 2)
-
-    def send_end_bias(g):
-        round_bias(1, g)
-        src = bias_out.at[1, :, :, pl.ds(g, 1)]
-        for off in range(2, group, 2):
-            bias_copy(1, g, src, me, far_sem.at[g], lax.rem(me + off, group)).start()
-        bias_copy(1, g, src, me, near_sem, twin).start()
-
-    def relay_bias(g):
-        wait_recv(bias_in.at[1, pl.ds(0, group // 2 - 1), :, :, pl.ds(g, 1)], far_sem.at[g])
-        for off in range(2, group, 2):
-            slot = lax.rem(me + off, group)
-            bias_copy(1, g, bias_in.at[1, slot, :, :, pl.ds(g, 1)], slot, near_sem, twin).start()
+        remote(src, bias_in.at[phase, slot, :, :, pl.ds(g, 1)], sem.at[phase, g], d).start()
+
+    def send_bias(phase, g, direct):
+        round_bias(phase, g)
+        src = bias_out.at[phase, :, :, pl.ds(g, 1)]
+        for off in range(1, group):
+            if off % 2 == 0:
+                bias_copy(phase, g, src, me, far_sem, lax.rem(me + off, group))
+            elif direct:
+                bias_copy(phase, g, src, me, near_sem, lax.rem(me + off, group))
+        if not direct:
+            bias_copy(phase, g, src, me, near_sem, twin)
+
+    def await_bias(phase, g, direct):
+        wait_recv(bias_in.at[phase, pl.ds(0, group // 2 - 1), :, :, pl.ds(g, 1)], far_sem.at[phase, g])
+        if not direct:
+            for off in range(2, group, 2):
+                slot = lax.rem(me + off, group)
+                bias_copy(phase, g, bias_in.at[phase, slot, :, :, pl.ds(g, 1)], slot, near_sem, twin)
+
+    def await_twin(phase, g):
+        wait_recv(bias_in.at[phase, pl.ds(0, group // 2), :, :, pl.ds(g, 1)], near_sem.at[phase, g])
 
     def start_norm():
         wb = w_b[0].astype(BF16)
@@ -137,8 +140,11 @@
 
             loop(8, row, 4)
             if g == 0:
+                for i, load in enumerate(loads):
+                    if i != 1:
+                        load.start()
                 pl.semaphore_wait(barrier, group - 1)
-            send_start_bias(g)
+            send_bias(0, g, g == sub - 1)
 
     def project(c, u, lo, width, wq):
         y = mm(u, wq)
@@ -156,7 +162,10 @@
             v_t[c, :, pl.ds(LANES, LANES)] = jnp.concatenate(twice, axis=0).astype(BF16).T
 
     def spread_start_bias():
-        wait_recv(bias_in.at[0, others], start_sem)
+        for g in range(sub):
+            await_bias(0, g, g == sub - 1)
+        for g in range(sub):
+            await_twin(0, g)
         for pair in range(heads // 2):
             t0, t1, t2 = [doubled(bias_in[0, :, pair, t].astype(F32).reshape(seq, LANES)).T for t in range(3)]
             even = jnp.concatenate([t0, t2[:tail]], axis=0)
@@ -165,16 +174,12 @@
             bias_t[pair, :, pl.ds(LANES, LANES)] = odd[:, :LANES]
             bias_t[2, :, pl.ds(pair * LANES, LANES)] = jnp.where(low, even[:, LANES:], odd[:, LANES:])
 
-    def spread_end_bias():
-        wait_recv(bias_in.at[1, pl.ds(0, group // 2)], near_sem)
+    def spread_end_bias(lo, count, place):
         for pair in range(heads // 2):
             for t in range(3):
-                b = bias_in[1, :, pair, t].astype(F32)
-                b = jnp.concatenate([b[:, :early // 8].reshape(LANES, LANES), b[:, early // 8:].reshape(tail, LANES)], axis=0)
-                if t < 2:
-                    bias_t[pair, :, pl.ds(t * LANES, LANES)] = b
-                else:
-                    bias_t[2, :, pl.ds(pair * LANES, LANES)] = b
+                b = bias_in[1, :, pair, t, pl.ds(lo, count)].astype(F32).reshape(group * count * 8, LANES)
+                tile, at = (pair, t * LANES) if t < 2 else (2, pair * LANES)
+                bias_t[tile, pl.ds(place, group * count * 8), pl.ds(at, LANES)] = b
 
     zero = jnp.zeros((dim, LANES), BF16)
     zero2 = jnp.zeros((2 * dim, LANES), BF16)
@@ -215,22 +220,25 @@
     def pipeline(stages, send):
         depth, count = len(stages), rows // 2
 
-        def turn(i, active):
+        def turn(i, active, eager=False):
             for stage in sorted(active, reverse=True):
                 for slot in range(2):
                     stages[stage](2 * (i - stage) + slot, slot)
-            send(i, active)
-
-        for i in range(depth - 1):
-            turn(i, range(i + 1))
+                if eager:
+                    send(i, (stage,))
+            if not eager:
+                send(i, active)
+
+        for i in range(depth):
+            turn(i, range(i + 1), True)
 
         def step(i, carry):
             turn(i, range(depth))
             return carry
 
-        lax.fori_loop(depth - 1, count, step, 0)
+        lax.fori_loop(depth, count, step, 0)
         for i in range(count, count + depth - 1):
-            turn(i, range(i - count + 1, depth))
+            turn(i, range(i - count + 1, depth), True)
 
     def score(r, slot):
         for t in range(3):
@@ -281,28 +289,32 @@
             r = 2 * (i - 3)
             if isinstance(r, int):
                 if r % 8 == 6:
-                    send_end_bias(r // 8)
+                    send_bias(1, r // 8, r // 8 == sub - 1)
             else:
                 @pl.when(lax.rem(r, 8) == 6)
                 def _():
-                    send_end_bias(r // 8)
+                    send_bias(1, r // 8, False)
 
     pipeline((score, mix, start_merge, end_bias), start_send)
 
     for g in range(sub - 1):
-        relay_bias(g)
+        await_bias(1, g, False)
     wait_recv(h_in.at[others, pl.ds(0, early)], h_sem.at[0])
     unpack(h_in, 0, early, 0)
 
     def end_project(lo, width):
         return lambda c: project(c, layer_norm(flat[pl.ds(lo * rows + c, width, stride=rows), :]), lo, width, wqe_ref[...])
 
-    loop(rows, end_project(0, LANES), 2)
+    loop(rows, end_project(0, LANES), 4)
+    for g in range(sub - 1):
+        await_twin(1, g)
+    spread_end_bias(0, early // 8, 0)
     wait_recv(h_in.at[others, pl.ds(early, rows - early)], h_sem.at[1])
-    relay_bias(sub - 1)
     unpack(h_in, early, rows - early, LANES * rows)
-    loop(rows, end_project(LANES, tail), 4)
-    spread_end_bias()
+    await_bias(1, sub - 1, True)
+    await_twin(1, sub - 1)
+    spread_end_bias(early // 8, sub - early // 8, LANES)
+    late_project = end_project(LANES, tail)
     column = lambda c: flat[pl.ds(c, seq, stride=rows), :]
 
     def by_owner(vals):
@@ -320,14 +332,14 @@
         normed[slot] = layer_norm(column(c) + upd)
 
     def transition(c, slot):
-        hidden = jnp.maximum(mm(normed[slot], w1_ref[...]), 0.0).astype(BF16)
+        hidden = jnp.maximum(mm(normed[slot], w1_ref[...]).astype(BF16), 0.0)
         d_out[c] = by_owner(upds[slot] + mm(hidden, w2_ref[...])).astype(BF16)
 
     def end_send(i, active):
-        if 3 in active:
-            send_rows(2 * (i - 3), d_out, d_in, lambda c: d_sem.at[c // 8])
-
-    pipeline((score, mix, end_merge, transition), end_send)
+        if 4 in active:
+            send_rows(2 * (i - 4), d_out, d_in, lambda c: d_sem.at[c // 8])
+
+    pipeline((lambda c, slot: late_project(c), score, mix, end_merge, transition), end_send)
     for g in range(sub):
         wait_recv(d_in.at[others, pl.ds(g * 8, 8)], d_sem.at[g])
 
@@ -384,9 +396,8 @@
             pltpu.SemaphoreType.DMA((sub,)),
             pltpu.SemaphoreType.DMA((len(weights),)),
             pltpu.SemaphoreType.DMA,
-            pltpu.SemaphoreType.DMA,
-            pltpu.SemaphoreType.DMA((sub,)),
-            pltpu.SemaphoreType.DMA,
+            pltpu.SemaphoreType.DMA((2, sub)),
+            pltpu.SemaphoreType.DMA((2, sub)),
             pltpu.SemaphoreType.DMA((2,)),
             pltpu.SemaphoreType.DMA((sub,)),
         ]

time: 53.5 us -> 50.4 us (0.942)
  Pallas kernels: 52 us -> 48.9 us
    pallas_call x1, Pallas kernels: 52 us -> 48.9 us  [local_fn(): pl.pallas_call(functools.partial(kernel, (group, rows, seq, chan, heads,...]
where the time goes in v5:
time: 50.4 us; the launch traced here: 50.3 us
  Pallas kernels  48.9 us (97%)
  local copies, waits for them, and re-layouts  1.41 us (3%)
    pallas_call x1, Pallas kernels, local_fn(): pl.pallas_call(functools.partial(kernel, (group, rows, seq, chan, heads,...  48.9 us
    unnamed x1, local copies, waits for them, and re-layouts  1.41 us

profile of v5, /device:TPU:81, one launch (start us, length us, event | category | flops | bytes accessed | tf_op | source)
XLA Modules:
  0.0 50.3 jit_solution(7341841994999388921)
XLA Ops:
  0.0 48.9 %shard_map.91 = f32[24,192,128]{2,1,0:T(8,128)S(1)} custom-call(f32[24,192,128]{2,1,0:T(8,128)} %z_hbm.1, bf16[128,512]{1,0:T(8,128)(2,1)} %wqs_hbm.1, bf16[4,128]{1,0:T(4,128)(2,1)} %wbs_hbm.1, bf16[128,128]{1,0:T(8,128)(2,1)} %wos_hbm.1, bf16[128,512]{1,0:T(8,128)(2,1)} %wqe_hbm.1, bf16[4,128]{1,0:T(4,128)(2,1)} %wbe_hbm.1, bf16[128,128]{1,0:T(8,128)(2,1)} %woe_hbm.1, ...), custom_call_target="tpu_custom_call" | custom-call | tf_op jit(solution)/shard_map/pallas_call | solution.py:404
  48.9 1.4 %copy.11 = f32[24,192,128]{2,1,0:T(8,128)} copy(f32[24,192,128]{2,1,0:T(8,128)S(1)} %shard_map.91) | data formatting | bytes 4718592

commit v6 on v5

--- a/solution.py
+++ b/solution.py
@@ -9,7 +9,6 @@
 
 LN_EPS = 1e-5
 LANES = 128
-SEND = 2
 F32, BF16 = jnp.float32, jnp.bfloat16
 
 
@@ -67,7 +66,7 @@
         return jnp.concatenate([rows_in, rows_in[LANES:seq]], axis=0)
 
     def peers(start):
-        for off in range(1, group):
+        for off in sorted(range(1, group), key=lambda o: abs(2 * o - group)):
             start(lax.rem(me + off, group))
 
     def remote(src, dst, recv, dst_dev):
@@ -144,7 +143,7 @@
                     if i != 1:
                         load.start()
                 pl.semaphore_wait(barrier, group - 1)
-            send_bias(0, g, g == sub - 1)
+            send_bias(0, g, True)
 
     def project(c, u, lo, width, wq):
         y = mm(u, wq)
@@ -163,7 +162,7 @@
 
     def spread_start_bias():
         for g in range(sub):
-            await_bias(0, g, g == sub - 1)
+            await_bias(0, g, True)
         for g in range(sub):
             await_twin(0, g)
         for pair in range(heads // 2):
@@ -217,45 +216,72 @@
         o = jnp.concatenate([o[:LANES], jnp.where(even_head, o[LANES:LANES + tail], o[LANES + tail:])], axis=0)
         return mm((o * gate[r]).astype(BF16), wo)
 
-    def pipeline(stages, send):
+    def pipeline(stages, send, sender, chunk):
         depth, count = len(stages), rows // 2
 
-        def turn(i, active, eager=False):
-            for stage in sorted(active, reverse=True):
-                for slot in range(2):
-                    stages[stage](2 * (i - stage) + slot, slot)
-                if eager:
-                    send(i, (stage,))
-            if not eager:
-                send(i, active)
-
-        for i in range(depth):
-            turn(i, range(i + 1), True)
-
-        def step(i, carry):
-            turn(i, range(depth))
+        def steps(i, parity, stage):
+            pair, half = i - stage, (parity + stage) % 2
+            return [part for slot in range(2) for part in stages[stage](2 * pair + slot, 2 * half + slot)]
+
+        def turn(i, parity, active):
+            light, heavy = [], []
+            for stage in active:
+                for part in steps(i, parity, stage):
+                    (light if stages[stage] in (score, mix) else heavy).append((part, stage))
+            light.sort(key=lambda entry: -entry[1])
+            mixes = [part for part, stage in light if stages[stage] is mix]
+            marks = [part for part, stage in light if stages[stage] is score]
+            light = [part for both in zip(mixes, marks) for part in both] if mixes and marks else mixes + marks
+            heavy = [part for part, _ in sorted(heavy, key=lambda entry: -entry[1])]
+            every = max(1, -(-len(light) // max(1, len(heavy))))
+            while light or heavy:
+                for part in heavy[:1] + light[:every]:
+                    part()
+                heavy, light = heavy[1:], light[every:]
+
+        def peeled(i):
+            active = [stage for stage in range(depth) if 0 <= i - stage < count]
+            if sender in active:
+                for part in steps(i, i % 2, sender):
+                    part()
+                send(i, 2, (sender,))
+                active.remove(sender)
+            turn(i, i % 2, active)
+            send(i, 2, active)
+
+        first = sender + 2
+        for i in range(first):
+            peeled(i)
+        base = first if first >= depth - 1 else depth - 1
+
+        def step(k, carry):
+            i = base + 2 * k
+            for j in range(2):
+                turn(i + j, (base + j) % 2, range(depth))
+                if chunk == 2:
+                    send(i + j, 2, range(depth))
+            if chunk == 4:
+                send(i, 4, range(depth))
             return carry
 
-        lax.fori_loop(depth, count, step, 0)
-        for i in range(count, count + depth - 1):
-            turn(i, range(i - count + 1, depth), True)
+        lax.fori_loop(0, (count - base) // 2, step, 0)
+        for i in range(base + (count - base) // 2 * 2, count + depth - 1):
+            peeled(i)
 
     def score(r, slot):
-        for t in range(3):
-            score_tile(r, slot, t)
+        return [functools.partial(score_tile, r, slot, t) for t in range(3)]
 
     def mix(r, slot):
-        for t in range(3):
-            mix_tile(r, slot, t)
-
-    def send_rows(first, src, dst, sem):
-        some = pl.ds(first, SEND)
+        return [functools.partial(mix_tile, r, slot, t) for t in range(3)]
+
+    def send_rows(first, size, src, dst, sem):
+        some = pl.ds(first, size)
         dst[me, some] = src[some, pl.ds(me * sub, sub)]
         peers(lambda d: remote(src.at[some, pl.ds(d * sub, sub)], dst.at[me, some], sem(first), d).start())
 
-    def unpack(src, lo, count, base):
+    def unpack(src, lo, base, stride):
         def part(d):
-            flat[pl.ds(base + d * count * rows, count * rows), :] = src[d, pl.ds(lo, count)].astype(F32).reshape(count * rows, chan)
+            flat[pl.ds((base + d * stride) * rows, 8 * rows), :] = src[d, pl.ds(lo, 8)].astype(F32).reshape(8 * rows, chan)
 
         loop(group, part)
 
@@ -282,35 +308,36 @@
         h = out_ref[r].astype(BF16).astype(F32)
         put_bias(r, w_b[1].astype(BF16), layer_norm(by_place(h)))
 
-    def start_send(i, active):
+    def start_send(i, size, active):
         if 2 in active:
-            send_rows(2 * (i - 2), h_out, h_in, lambda r: h_sem.at[r // early])
+            send_rows(2 * (i - 2), size, h_out, h_in, lambda r: h_sem.at[r // 8])
         if 3 in active:
-            r = 2 * (i - 3)
-            if isinstance(r, int):
-                if r % 8 == 6:
-                    send_bias(1, r // 8, r // 8 == sub - 1)
+            pair = i - 3
+            if isinstance(pair, int):
+                if pair % 4 == 3:
+                    send_bias(1, pair // 4, pair // 4 == sub - 1)
             else:
-                @pl.when(lax.rem(r, 8) == 6)
+                @pl.when(lax.rem(pair, 4) == 3)
                 def _():
-                    send_bias(1, r // 8, False)
-
-    pipeline((score, mix, start_merge, end_bias), start_send)
-
+                    send_bias(1, pair // 4, False)
+
+    pipeline((score, mix, lambda r, slot: [lambda: start_merge(r, slot)], lambda r, slot: [lambda: end_bias(r, slot)]), start_send, 2, 4)
+
+    for g in range(sub - 1):
+        wait_recv(h_in.at[others, pl.ds(g * 8, 8)], h_sem.at[g])
+        unpack(h_in, g * 8, g * 8, early)
+
+    def end_project(lo, width):
+        return lambda c: project(c, layer_norm(flat[pl.ds(lo * rows + c, width, stride=rows), :]), lo, width, wqe_ref[...])
+
+    loop(rows, end_project(0, LANES), 4)
     for g in range(sub - 1):
         await_bias(1, g, False)
-    wait_recv(h_in.at[others, pl.ds(0, early)], h_sem.at[0])
-    unpack(h_in, 0, early, 0)
-
-    def end_project(lo, width):
-        return lambda c: project(c, layer_norm(flat[pl.ds(lo * rows + c, width, stride=rows), :]), lo, width, wqe_ref[...])
-
-    loop(rows, end_project(0, LANES), 4)
+    wait_recv(h_in.at[others, pl.ds(early, 8)], h_sem.at[sub - 1])
+    unpack(h_in, early, LANES, 8)
     for g in range(sub - 1):
         await_twin(1, g)
     spread_end_bias(0, early // 8, 0)
-    wait_recv(h_in.at[others, pl.ds(early, rows - early)], h_sem.at[1])
-    unpack(h_in, early, rows - early, LANES * rows)
     await_bias(1, sub - 1, True)
     await_twin(1, sub - 1)
     spread_end_bias(early // 8, sub - early // 8, LANES)
@@ -335,11 +362,12 @@
         hidden = jnp.maximum(mm(normed[slot], w1_ref[...]).astype(BF16), 0.0)
         d_out[c] = by_owner(upds[slot] + mm(hidden, w2_ref[...])).astype(BF16)
 
-    def end_send(i, active):
+    def end_send(i, size, active):
         if 4 in active:
-            send_rows(2 * (i - 4), d_out, d_in, lambda c: d_sem.at[c // 8])
-
-    pipeline((lambda c, slot: late_project(c), score, mix, end_merge, transition), end_send)
+            send_rows(2 * (i - 4), size, d_out, d_in, lambda c: d_sem.at[c // 8])
+
+    pipeline((lambda c, slot: [lambda: late_project(c)], score, mix, lambda c, slot: [lambda: end_merge(c, slot)],
+              lambda c, slot: [lambda: transition(c, slot)]), end_send, 4, 2)
     for g in range(sub):
         wait_recv(d_in.at[others, pl.ds(g * 8, 8)], d_sem.at[g])
 
@@ -384,11 +412,11 @@
             pltpu.VMEM((2, heads // 2, 3, sub, 8, LANES), BF16),
             pltpu.VMEM((2, group, heads // 2, 3, sub, 8, LANES), BF16),
             pltpu.VMEM((3, seq, packed), F32),
-            pltpu.VMEM((2, 3, seq, packed), F32),
-            pltpu.VMEM((2, 3, 1, packed), F32),
-            pltpu.VMEM((2, chan, packed), F32),
-            pltpu.VMEM((2, seq, chan), F32),
-            pltpu.VMEM((2, seq, chan), BF16),
+            pltpu.VMEM((4, 3, seq, packed), F32),
+            pltpu.VMEM((4, 3, 1, packed), F32),
+            pltpu.VMEM((4, chan, packed), F32),
+            pltpu.VMEM((4, seq, chan), F32),
+            pltpu.VMEM((4, seq, chan), BF16),
             pltpu.VMEM((rows, seq // 8, 8, chan), BF16),
             pltpu.VMEM((group, rows, sub, 8, chan), BF16),
             pltpu.VMEM((rows, seq // 8, 8, chan), BF16),
@@ -398,7 +426,7 @@
             pltpu.SemaphoreType.DMA,
             pltpu.SemaphoreType.DMA((2, sub)),
             pltpu.SemaphoreType.DMA((2, sub)),
-            pltpu.SemaphoreType.DMA((2,)),
+            pltpu.SemaphoreType.DMA((sub,)),
             pltpu.SemaphoreType.DMA((sub,)),
         ]
         return pl.pallas_call(

time: 50.4 us -> 49.6 us (0.984)
  Pallas kernels: 48.9 us -> 48.1 us
    pallas_call x1, Pallas kernels: 48.9 us -> 48.1 us  [local_fn(): pl.pallas_call(functools.partial(kernel, (group, rows, seq, chan, heads,...]
where the time goes in v6:
time: 49.6 us; the launch traced here: 49.5 us
  Pallas kernels  48.1 us (97%)
  local copies, waits for them, and re-layouts  1.41 us (3%)
    pallas_call x1, Pallas kernels, local_fn(): pl.pallas_call(functools.partial(kernel, (group, rows, seq, chan, heads,...  48.1 us
    unnamed x1, local copies, waits for them, and re-layouts  1.41 us

profile of v6, /device:TPU:81, one launch (start us, length us, event | category | flops | bytes accessed | tf_op | source)
XLA Modules:
  0.0 49.5 jit_solution(8853165286163246902)
XLA Ops:
  0.0 48.1 %shard_map.91 = f32[24,192,128]{2,1,0:T(8,128)S(1)} custom-call(f32[24,192,128]{2,1,0:T(8,128)} %z_hbm.1, bf16[128,512]{1,0:T(8,128)(2,1)} %wqs_hbm.1, bf16[4,128]{1,0:T(4,128)(2,1)} %wbs_hbm.1, bf16[128,128]{1,0:T(8,128)(2,1)} %wos_hbm.1, bf16[128,512]{1,0:T(8,128)(2,1)} %wqe_hbm.1, bf16[4,128]{1,0:T(4,128)(2,1)} %wbe_hbm.1, bf16[128,128]{1,0:T(8,128)(2,1)} %woe_hbm.1, ...), custom_call_target="tpu_custom_call" | custom-call | tf_op jit(solution)/shard_map/pallas_call | solution.py:432
  48.1 1.4 %copy.11 = f32[24,192,128]{2,1,0:T(8,128)} copy(f32[24,192,128]{2,1,0:T(8,128)S(1)} %shard_map.91) | data formatting | bytes 4718592

commit v7 on v6

--- a/solution.py
+++ b/solution.py
@@ -199,6 +199,16 @@
         scores[slot, t] = s
         tops[slot, t] = jnp.max(s, axis=0, keepdims=True)
 
+    def raw_tiles(rs):
+        for slot, r in enumerate(rs):
+            for t in range(3):
+                scores[slot, t] = mm(keys[r], query_tile(r, t)) * scale
+
+    def biased_tile(slot, t):
+        s = scores[slot, t] + bias_t[t]
+        scores[slot, t] = s
+        tops[slot, t] = jnp.max(s, axis=0, keepdims=True)
+
     def mix_tile(r, slot, t):
         e = jnp.exp(scores[slot, t] - tops[slot, t])
         total = jnp.sum(e, axis=0, keepdims=True)
@@ -216,11 +226,15 @@
         o = jnp.concatenate([o[:LANES], jnp.where(even_head, o[LANES:LANES + tail], o[LANES + tail:])], axis=0)
         return mm((o * gate[r]).astype(BF16), wo)
 
-    def pipeline(stages, send, sender, chunk):
+    def pipeline(stages, send, sender, chunk, done=()):
         depth, count = len(stages), rows // 2
 
         def steps(i, parity, stage):
             pair, half = i - stage, (parity + stage) % 2
+            if isinstance(pair, int) and (stage, pair) in done:
+                return []
+            if isinstance(pair, int) and pair == 0 and stages[stage] is score:
+                return [functools.partial(biased_tile, slot, t) for slot in range(2) for t in range(3)]
             return [part for slot in range(2) for part in stages[stage](2 * pair + slot, 2 * half + slot)]
 
         def turn(i, parity, active):
@@ -297,6 +311,7 @@
     for load in loads[2:]:
         load.wait()
     load_bias_weight(1, wbe_ref)
+    raw_tiles((0, 1))
     spread_start_bias()
 
     def start_merge(r, slot):
@@ -335,13 +350,16 @@
         await_bias(1, g, False)
     wait_recv(h_in.at[others, pl.ds(early, 8)], h_sem.at[sub - 1])
     unpack(h_in, early, LANES, 8)
+    late_project = end_project(LANES, tail)
+    for c in range(4):
+        late_project(c)
+    raw_tiles((0, 1))
     for g in range(sub - 1):
         await_twin(1, g)
     spread_end_bias(0, early // 8, 0)
     await_bias(1, sub - 1, True)
     await_twin(1, sub - 1)
     spread_end_bias(early // 8, sub - early // 8, LANES)
-    late_project = end_project(LANES, tail)
     column = lambda c: flat[pl.ds(c, seq, stride=rows), :]
 
     def by_owner(vals):
@@ -367,7 +385,7 @@
             send_rows(2 * (i - 4), size, d_out, d_in, lambda c: d_sem.at[c // 8])
 
     pipeline((lambda c, slot: [lambda: late_project(c)], score, mix, lambda c, slot: [lambda: end_merge(c, slot)],
-              lambda c, slot: [lambda: transition(c, slot)]), end_send, 4, 2)
+              lambda c, slot: [lambda: transition(c, slot)]), end_send, 4, 2, ((0, 0), (0, 1)))
     for g in range(sub):
         wait_recv(d_in.at[others, pl.ds(g * 8, 8)], d_sem.at[g])
 

time: 49.6 us -> 49.2 us (level)
  no operation moved by 1% of the time
where the time goes in v7:
time: 49.2 us; the launch traced here: 49.1 us
  Pallas kernels  47.7 us (97%)
  local copies, waits for them, and re-layouts  1.41 us (3%)
    pallas_call x1, Pallas kernels, local_fn(): pl.pallas_call(functools.partial(kernel, (group, rows, seq, chan, heads,...  47.7 us
    unnamed x1, local copies, waits for them, and re-layouts  1.41 us

profile of v7, /device:TPU:81, one launch (start us, length us, event | category | flops | bytes accessed | tf_op | source)
XLA Modules:
  0.0 49.1 jit_solution(3268387792370071481)
XLA Ops:
  0.0 47.7 %shard_map.91 = f32[24,192,128]{2,1,0:T(8,128)S(1)} custom-call(f32[24,192,128]{2,1,0:T(8,128)} %z_hbm.1, bf16[128,512]{1,0:T(8,128)(2,1)} %wqs_hbm.1, bf16[4,128]{1,0:T(4,128)(2,1)} %wbs_hbm.1, bf16[128,128]{1,0:T(8,128)(2,1)} %wos_hbm.1, bf16[128,512]{1,0:T(8,128)(2,1)} %wqe_hbm.1, bf16[4,128]{1,0:T(4,128)(2,1)} %wbe_hbm.1, bf16[128,128]{1,0:T(8,128)(2,1)} %woe_hbm.1, ...), custom_call_target="tpu_custom_call" | custom-call | tf_op jit(solution)/shard_map/pallas_call | solution.py:450
  47.7 1.4 %copy.11 = f32[24,192,128]{2,1,0:T(8,128)} copy(f32[24,192,128]{2,1,0:T(8,128)S(1)} %shard_map.91) | data formatting | bytes 4718592

commit v8 on v7

--- a/solution.py
+++ b/solution.py
@@ -137,7 +137,7 @@
                 norm[r] = u
                 put_bias(r, wb, u)
 
-            loop(8, row, 4)
+            loop(8, row, 8)
             if g == 0:
                 for i, load in enumerate(loads):
                     if i != 1:
@@ -336,7 +336,7 @@
                 def _():
                     send_bias(1, pair // 4, False)
 
-    pipeline((score, mix, lambda r, slot: [lambda: start_merge(r, slot)], lambda r, slot: [lambda: end_bias(r, slot)]), start_send, 2, 4)
+    pipeline((score, mix, lambda r, slot: [lambda: start_merge(r, slot)], lambda r, slot: [lambda: end_bias(r, slot)]), start_send, 2, 2)
 
     for g in range(sub - 1):
         wait_recv(h_in.at[others, pl.ds(g * 8, 8)], h_sem.at[g])

time: 49.2 us -> 48.7 us (0.990)
  Pallas kernels: 47.7 us -> 47.2 us
    pallas_call x1, Pallas kernels: 47.7 us -> 47.2 us  [local_fn(): pl.pallas_call(functools.partial(kernel, (group, rows, seq, chan, heads,...]
where the time goes in v8:
time: 48.7 us; the launch traced here: 48.6 us
  Pallas kernels  47.2 us (97%)
  local copies, waits for them, and re-layouts  1.41 us (3%)
    pallas_call x1, Pallas kernels, local_fn(): pl.pallas_call(functools.partial(kernel, (group, rows, seq, chan, heads,...  47.2 us
    unnamed x1, local copies, waits for them, and re-layouts  1.41 us

profile of v8, /device:TPU:81, one launch (start us, length us, event | category | flops | bytes accessed | tf_op | source)
XLA Modules:
  0.0 48.6 jit_solution(10451969319555547948)
XLA Ops:
  0.0 47.2 %shard_map.91 = f32[24,192,128]{2,1,0:T(8,128)S(1)} custom-call(f32[24,192,128]{2,1,0:T(8,128)} %z_hbm.1, bf16[128,512]{1,0:T(8,128)(2,1)} %wqs_hbm.1, bf16[4,128]{1,0:T(4,128)(2,1)} %wbs_hbm.1, bf16[128,128]{1,0:T(8,128)(2,1)} %wos_hbm.1, bf16[128,512]{1,0:T(8,128)(2,1)} %wqe_hbm.1, bf16[4,128]{1,0:T(4,128)(2,1)} %wbe_hbm.1, bf16[128,128]{1,0:T(8,128)(2,1)} %woe_hbm.1, ...), custom_call_target="tpu_custom_call" | custom-call | tf_op jit(solution)/shard_map/pallas_call | solution.py:450
  47.2 1.4 %copy.11 = f32[24,192,128]{2,1,0:T(8,128)} copy(f32[24,192,128]{2,1,0:T(8,128)S(1)} %shard_map.91) | data formatting | bytes 4718592

commit v9 on v8

--- a/solution.py
+++ b/solution.py
@@ -297,7 +297,7 @@
         def part(d):
             flat[pl.ds((base + d * stride) * rows, 8 * rows), :] = src[d, pl.ds(lo, 8)].astype(F32).reshape(8 * rows, chan)
 
-        loop(group, part)
+        loop(group, part, 4)
 
     def by_place(vals):
         parts = vals.reshape(group, sub, 8, chan)
@@ -392,14 +392,14 @@
         def part(d):
             flat[pl.ds((d * rows + g * 8) * rows, 8 * rows), :] = d_in[d, pl.ds(g * 8, 8)].astype(F32).reshape(8 * rows, chan)
 
-        loop(group, part, 2)
+        loop(group, part, 4)
 
         def final(r):
             for d in range(group):
                 at = d * rows + g * 8
                 out_ref[r, pl.ds(at, 8), :] = out_ref[r, pl.ds(at, 8), :] + flat[pl.ds(at * rows + r, 8, stride=rows), :]
 
-        loop(rows, final, 4)
+        loop(rows, final, 8)
 
     for phase in range(2):
         wait_send(bias_in.at[phase, others])

time: 48.7 us -> 48.7 us (level)
  no operation moved by 1% of the time
where the time goes in v9:
time: 48.7 us; the launch traced here: 48.6 us
  Pallas kernels  47.2 us (97%)
  local copies, waits for them, and re-layouts  1.41 us (3%)
    pallas_call x1, Pallas kernels, local_fn(): pl.pallas_call(functools.partial(kernel, (group, rows, seq, chan, heads,...  47.2 us
    unnamed x1, local copies, waits for them, and re-layouts  1.41 us

profile of v9, /device:TPU:81, one launch (start us, length us, event | category | flops | bytes accessed | tf_op | source)
XLA Modules:
  0.0 48.6 jit_solution(4315680712609651187)
XLA Ops:
  0.0 47.2 %shard_map.91 = f32[24,192,128]{2,1,0:T(8,128)S(1)} custom-call(f32[24,192,128]{2,1,0:T(8,128)} %z_hbm.1, bf16[128,512]{1,0:T(8,128)(2,1)} %wqs_hbm.1, bf16[4,128]{1,0:T(4,128)(2,1)} %wbs_hbm.1, bf16[128,128]{1,0:T(8,128)(2,1)} %wos_hbm.1, bf16[128,512]{1,0:T(8,128)(2,1)} %wqe_hbm.1, bf16[4,128]{1,0:T(4,128)(2,1)} %wbe_hbm.1, bf16[128,128]{1,0:T(8,128)(2,1)} %woe_hbm.1, ...), custom_call_target="tpu_custom_call" | custom-call | tf_op jit(solution)/shard_map/pallas_call | solution.py:450
  47.2 1.4 %copy.11 = f32[24,192,128]{2,1,0:T(8,128)} copy(f32[24,192,128]{2,1,0:T(8,128)S(1)} %shard_map.91) | data formatting | bytes 4718592
